TPU v7x, 64 devices: a 2x2x8 block of a 4x4x8 slice. The times are simulated.
64 devices in a mesh: dp: 4 (over x, y), sp: 16 (over z, core).
Axes of the slice: x: 2, y: 2, z: 8, core: 2. Of those that a mesh axis runs over, the one named last changes fastest.
The devices are a block of a 4x4x8 slice.
Arguments:
- hidden: bfloat16 [1024, 4096], P(('dp', 'sp')), parts along dimension 0
- w_q: bfloat16 [4096, 12288], replicated
- w_k: bfloat16 [4096, 1024], replicated
- w_v: bfloat16 [4096, 1024], replicated
- w_o: bfloat16 [12288, 4096], replicated
- expert_ids: int32 [1024, 2], P(('dp', 'sp')), parts along dimension 0
- router_probs: float32 [1024, 128], P(('dp', 'sp')), parts along dimension 0
Outputs:
- output 1: bfloat16 [1024, 4096], P(('dp', 'sp')), parts along dimension 0
- output 2: bfloat16 [512, 256, 4096], P(('dp', 'sp')), parts along dimension 0
There are 4 independent parts. A program takes and returns all parts, laid end to end along the dimension named above; an argument that names none is the same for every part.
All inputs are finite; a program needn't handle non-finite values.
Results may differ from a plain program's by a relative error of at most 0.00852087.
Values are sent between devices in bfloat16 or wider.
A program may use at most 768 MiB of HBM per device.

v0:
```python
import math
import jax
import jax.numpy as jnp
from jax import lax
from jax.sharding import PartitionSpec as P

HEAD_DIM = 128
SCORE_SCALE = 1.0 / math.sqrt(HEAD_DIM)


def route_rows(hidden_out, expert_ids, router_probs):
    tok_dev, width = hidden_out.shape
    experts = router_probs.shape[1]
    picked = jnp.take_along_axis(router_probs, expert_ids, axis=1)
    gate_w = picked / jnp.sum(picked, axis=1, keepdims=True)
    gated = (gate_w[:, :, None] * hidden_out[:, None, :].astype(jnp.float32)).astype(jnp.bfloat16)
    token_hits = jnp.sum((expert_ids[:, :, None] == jnp.arange(experts)).astype(jnp.int32), axis=1)
    earlier = jnp.cumsum(token_hits, axis=0) - token_hits
    slot_rank = jnp.take_along_axis(earlier, expert_ids, axis=1)
    send_buf = jnp.zeros((experts, tok_dev, width), jnp.bfloat16)
    return send_buf.at[expert_ids, slot_rank].set(gated, unique_indices=True)


def solution(mesh):
    group = mesh.shape['sp']
    row_spec = P(('dp', 'sp'), None)
    buf_spec = P(('dp', 'sp'), None, None)

    def device_step(x_loc, w_q, w_k, w_v, w_o, ids_loc, probs_loc):
        tok_dev = x_loc.shape[0]
        seq_len = tok_dev * group
        n_heads = w_q.shape[1] // HEAD_DIM
        kv_heads = w_k.shape[1] // HEAD_DIM
        kv_copies = max(1, group // kv_heads)
        head_dev = n_heads // group
        kv_dev = kv_heads * kv_copies // group
        q_loc = jnp.dot(x_loc, w_q, preferred_element_type=jnp.float32).astype(jnp.bfloat16).reshape(tok_dev, n_heads, HEAD_DIM)
        k_loc = jnp.dot(x_loc, w_k, preferred_element_type=jnp.float32).astype(jnp.bfloat16).reshape(tok_dev, kv_heads, HEAD_DIM)
        v_loc = jnp.dot(x_loc, w_v, preferred_element_type=jnp.float32).astype(jnp.bfloat16).reshape(tok_dev, kv_heads, HEAD_DIM)
        k_loc = jnp.repeat(k_loc, kv_copies, axis=1)
        v_loc = jnp.repeat(v_loc, kv_copies, axis=1)
        q_seq = lax.all_to_all(q_loc, 'sp', 1, 0, tiled=True)
        k_seq = lax.all_to_all(k_loc, 'sp', 1, 0, tiled=True)
        v_seq = lax.all_to_all(v_loc, 'sp', 1, 0, tiled=True)
        q_grp = q_seq.reshape(seq_len, kv_dev, head_dev // kv_dev, HEAD_DIM)
        scores = jnp.einsum('qgmd,kgd->gmqk', q_grp, k_seq, preferred_element_type=jnp.float32) * SCORE_SCALE
        positions = jnp.arange(seq_len)
        causal = positions[:, None] >= positions[None, :]
        weights = jax.nn.softmax(jnp.where(causal, scores, -1e30), axis=-1).astype(jnp.bfloat16)
        attn_seq = jnp.einsum('gmqk,kgd->qgmd', weights, v_seq, preferred_element_type=jnp.float32).astype(jnp.bfloat16)
        attn_seq = attn_seq.reshape(seq_len, head_dev, HEAD_DIM)
        attn_loc = lax.all_to_all(attn_seq, 'sp', 0, 1, tiled=True).reshape(tok_dev, n_heads * HEAD_DIM)
        out_proj = jnp.dot(attn_loc, w_o, preferred_element_type=jnp.float32)
        hidden_out = (x_loc.astype(jnp.float32) + out_proj).astype(jnp.bfloat16)
        send_buf = route_rows(hidden_out, ids_loc, probs_loc)
        recv_buf = lax.all_to_all(send_buf, 'sp', 0, 1, tiled=True)
        return hidden_out, recv_buf

    return jax.shard_map(device_step, mesh=mesh, in_specs=(row_spec, P(), P(), P(), P(), row_spec, row_spec), out_specs=(row_spec, buf_spec), check_vma=False)
```

profile of v0, /device:TPU:21, one launch (start us, length us, event | category | flops | bytes accessed | tf_op | source)
XLA Modules:
  0.0 532.7 jit_solution(3611111712348963029)
XLA Ops:
  0.6 0.0 copy-start
  0.6 0.0 copy-start.2
  0.7 38.0 %fusion.3 = bf16[2,96,8,128]{3,2,1,0:T(8,128)(2,1)S(1)} fusion(bf16[16,4096]{1,0:T(8,128)(2,1)} %param.7, bf16[4096,12288]{1,0:T(8,128)(2,1)} %param.8), kind=kOutput, calls=%fused_computation.12 | convolution fusion | flops 1610809344 | bytes 101187584 | tf_op jit(solution)/shard_map/dot_general | solution.py:37
  38.7 0.8 copy.124
  39.5 10.7 %all-to-all-start.2 = ((bf16[16,96,128]{2,0,1:T(8,128)(2,1)}), bf16[16,96,128]{2,0,1:T(8,128)(2,1)S(1)}, u32[]{:S(2)}, u32[]{:S(2)}) async-start(bf16[16,96,128]{2,0,1:T(8,128)(2,1)} %bitcast.74), calls=%async_computation.2 | async-start | bytes 786432 | tf_op jit(solution)/shard_map/all_to_all | solution.py:42
  50.2 0.0 copy-done.2
  50.2 4.6 fusion.5
  54.8 9.5 %all-to-all-done.2 = bf16[16,96,128]{2,0,1:T(8,128)(2,1)S(1)} async-done(((bf16[16,96,128]{2,0,1:T(8,128)(2,1)}), bf16[16,96,128]{2,0,1:T(8,128)(2,1)S(1)}, u32[]{:S(2)}, u32[]{:S(2)}) %all-to-all-start.2) | async-done | bytes 393248 | tf_op jit(solution)/shard_map/all_to_all | solution.py:42
  64.3 0.6 broadcast_in_dim.40
  65.0 3.7 all-to-all-start.1
  68.6 4.6 fusion.4
  73.2 0.0 copy-start.3
  73.3 2.3 all-to-all-done.1
  75.6 0.6 broadcast_in_dim.38
  76.3 4.5 all-to-all-start
  80.8 0.4 fusion.11
  81.2 0.2 fusion.1
  81.4 6.8 %all-to-all-done = bf16[16,16,128]{2,0,1:T(8,128)(2,1)S(1)} async-done(((bf16[16,16,128]{2,0,1:T(8,128)(2,1)}), bf16[16,16,128]{2,0,1:T(8,128)(2,1)S(1)}, u32[]{:S(2)}, u32[]{:S(2)}) %all-to-all-start) | async-done | bytes 65568 | tf_op jit(solution)/shard_map/all_to_all | solution.py:44
  88.2 0.4 fusion.2
  88.6 1.1 copy.105
  89.7 3.9 all-to-all-start.3
  93.6 0.0 copy-done.3
  93.6 0.1 copy.108
  93.7 0.1 reshape.97
  93.8 0.0 copy-done
  93.8 0.7 gather_fusion.1
  94.5 0.1 reshape.106
  94.6 0.1 copy.111
  94.7 0.1 copy.112
  94.8 0.1 convert_reduce_fusion
  94.9 0.7 gather_fusion
  95.7 0.1 reshape.100
  95.7 0.1 copy.109
  95.9 0.1 copy.110
  95.9 0.1 reshape.109
  96.0 14.4 %all-to-all-done.3 = bf16[256,6,128]{2,1,0:T(8,128)(2,1)S(1)} async-done(((bf16[256,6,128]{2,1,0:T(8,128)(2,1)}), bf16[256,6,128]{2,1,0:T(8,128)(2,1)S(1)}, u32[]{:S(2)}, u32[]{:S(2)}) %all-to-all-start.3) | async-done | bytes 393248 | tf_op jit(solution)/shard_map/all_to_all | solution.py:52
  110.4 0.1 copy.107
  110.5 0.4 reshape.96
  111.0 33.9 %fusion.12 = (f32[16,4096]{1,0:T(8,128)S(1)}, bf16[16,4096]{1,0:T(8,128)(2,1)}) fusion(bf16[16,12288]{1,0:T(8,128)(2,1)S(1)} %reshape.96, bf16[12288,4096]{1,0:T(8,128)(2,1)} %param.11, bf16[16,4096]{1,0:T(8,128)(2,1)S(1)} %copy-done.2), kind=kOutput, calls=%fused_computation.39 | convolution fusion | flops 1610874880 | bytes 101580800 | tf_op jit(solution)/shard_map/dot_general | solution.py:53
  144.9 0.3 multiply_convert_fusion
  145.2 0.1 reshape.111
  145.3 6.1 %broadcast_in_dim.42 = bf16[128,16,4096]{2,1,0:T(8,128)(2,1)} broadcast(bf16[]{:T(256)} %constant.25.clone.1), dimensions={} | broadcast | bytes 16777218 | tf_op jit(solution)/shard_map/broadcast_in_dim | solution.py:20
  151.4 9.0 %scatter_fusion = bf16[128,16,4096]{2,1,0:T(8,128)(2,1)} fusion(bf16[128,16,4096]{2,1,0:T(8,128)(2,1)} %broadcast_in_dim.42, s32[32]{0:T(128)S(1)} %reshape.109, bf16[32,4096]{1,0:T(8,128)(2,1)S(1)} %reshape.111), kind=kCustom, calls=%fused_computation.2 | custom fusion | bytes 786688 | tf_op jit(solution)/shard_map/scatter | solution.py:21
  160.4 365.8 %all_to_all.78 = bf16[128,16,4096]{2,1,0:T(8,128)(2,1)S(1)} all-to-all(bf16[128,16,4096]{2,1,0:T(8,128)(2,1)} %scatter_fusion), channel_id=1, replica_groups=mesh['dp'=4,'sp'=16] {'sp'}, dimensions={0} | all-to-all | bytes 33554432 | tf_op jit(solution)/shard_map/all_to_all | solution.py:56
  526.2 0.0 copy-start.1
  526.2 6.5 %copy.113 = bf16[8,16,16,4096]{3,2,1,0:T(8,128)(2,1)} copy(bf16[8,16,16,4096]{3,2,0,1:T(8,128)(2,1)S(1)} %bitcast.78) | data formatting | bytes 33554432 | tf_op jit(solution)/shard_map/all_to_all | solution.py:56
  532.7 0.0 copy-done.1
  (10 shorter events, 0.2 us)
Async XLA Ops:
  0.6 93.2 %copy-start = (f32[16,128]{1,0:T(8,128)S(1)}, f32[16,128]{1,0:T(8,128)}, u32[]{:S(2)}) copy-start(f32[16,128]{1,0:T(8,128)} %param.13) | copy-start | bytes 24580
  0.6 49.6 %copy-start.2 = (bf16[16,4096]{1,0:T(8,128)(2,1)S(1)}, bf16[16,4096]{1,0:T(8,128)(2,1)}, u32[]{:S(2)}) copy-start(bf16[16,4096]{1,0:T(8,128)(2,1)} %param.7) | copy-start | bytes 393220
  39.5 24.8 %all-to-all-start.2 = ((bf16[16,96,128]{2,0,1:T(8,128)(2,1)}), bf16[16,96,128]{2,0,1:T(8,128)(2,1)S(1)}, u32[]{:S(2)}, u32[]{:S(2)}) async-start(bf16[16,96,128]{2,0,1:T(8,128)(2,1)} %bitcast.74), calls=%async_computation.2 | async-start | bytes 786432 | tf_op jit(solution)/shard_map/all_to_all | solution.py:42
  65.0 10.6 %all-to-all-start.1 = ((bf16[16,16,128]{2,0,1:T(8,128)(2,1)}), bf16[16,16,128]{2,0,1:T(8,128)(2,1)S(1)}, u32[]{:S(2)}, u32[]{:S(2)}) async-start(bf16[16,16,128]{2,0,1:T(8,128)(2,1)} %bitcast.5), calls=%async_computation.1 | async-start | bytes 131072 | tf_op jit(solution)/shard_map/all_to_all | solution.py:43
  73.2 20.4 %copy-start.3 = (s32[16,2]{0,1:T(2,128)S(1)}, s32[16,2]{0,1:T(2,128)}, u32[]{:S(2)}) copy-start(s32[16,2]{0,1:T(2,128)} %param.12) | copy-start | bytes 388
  76.3 11.9 %all-to-all-start = ((bf16[16,16,128]{2,0,1:T(8,128)(2,1)}), bf16[16,16,128]{2,0,1:T(8,128)(2,1)S(1)}, u32[]{:S(2)}, u32[]{:S(2)}) async-start(bf16[16,16,128]{2,0,1:T(8,128)(2,1)} %bitcast), calls=%async_computation | async-start | bytes 131072 | tf_op jit(solution)/shard_map/all_to_all | solution.py:44
  89.7 20.7 %all-to-all-start.3 = ((bf16[256,6,128]{2,1,0:T(8,128)(2,1)}), bf16[256,6,128]{2,1,0:T(8,128)(2,1)S(1)}, u32[]{:S(2)}, u32[]{:S(2)}) async-start(bf16[256,6,128]{2,1,0:T(8,128)(2,1)} %copy.105), calls=%async_computation.3 | async-start | bytes 1048576 | tf_op jit(solution)/shard_map/all_to_all | solution.py:52
  526.2 6.5 %copy-start.1 = (f32[16,128]{1,0:T(8,128)S(1)}, f32[16,128]{1,0:T(8,128)}, u32[]{:S(2)}) copy-start(f32[16,128]{1,0:T(8,128)} %param.13) | copy-start | bytes 24580
where the time goes:
time: 535 us; the launch traced here: 533 us
  blocking collectives  366 us (68%)
  matrix products  81.9 us (15%)
  waiting for transfers between devices  33 us (6%)
  local copies, waits for them, and re-layouts  27.7 us (5%)
  starting transfers between devices  22.8 us (4%)
    all_to_all x1, blocking collectives, device_step(): recv_buf = lax.all_to_all(send_buf, 'sp', 0, 1, tiled=True)  366 us
    dot_general x1, matrix products, device_step(): jnp.dot(x_loc, w_q, preferred_element_type=jnp.float32).astype(jnp.bfloat16)  38 us
    dot_general x1, matrix products, device_step(): out_proj = jnp.dot(attn_loc, w_o, preferred_element_type=jnp.float32)  33.9 us
    all_to_all x1, waiting for transfers between devices, device_step(): lax.all_to_all(attn_seq, 'sp', 0, 1, tiled=True)  14.4 us
    all_to_all x1, starting transfers between devices, device_step(): q_seq = lax.all_to_all(q_loc, 'sp', 1, 0, tiled=True)  10.7 us
  transfers between devices with their start and end apart: 4, of which 4 were waited for; matrix products, arithmetic and copies ran while one was open for 2% of the time, Pallas kernels for 0%

commit v1 on v0

--- a/solution.py
+++ b/solution.py
@@ -1,24 +1,102 @@
 import math
+import functools
 import jax
 import jax.numpy as jnp
 from jax import lax
+from jax.experimental import pallas as pl
+from jax.experimental.pallas import tpu as pltpu
 from jax.sharding import PartitionSpec as P
 
 HEAD_DIM = 128
 SCORE_SCALE = 1.0 / math.sqrt(HEAD_DIM)
+COLS = 256
 
 
-def route_rows(hidden_out, expert_ids, router_probs):
-    tok_dev, width = hidden_out.shape
-    experts = router_probs.shape[1]
-    picked = jnp.take_along_axis(router_probs, expert_ids, axis=1)
-    gate_w = picked / jnp.sum(picked, axis=1, keepdims=True)
-    gated = (gate_w[:, :, None] * hidden_out[:, None, :].astype(jnp.float32)).astype(jnp.bfloat16)
-    token_hits = jnp.sum((expert_ids[:, :, None] == jnp.arange(experts)).astype(jnp.int32), axis=1)
-    earlier = jnp.cumsum(token_hits, axis=0) - token_hits
-    slot_rank = jnp.take_along_axis(earlier, expert_ids, axis=1)
-    send_buf = jnp.zeros((experts, tok_dev, width), jnp.bfloat16)
-    return send_buf.at[expert_ids, slot_rank].set(gated, unique_indices=True)
+def route_table(me, ids, probs, seq, table_rows):
+    tok_dev, experts = probs.shape
+    lanes = experts
+    per_row = lanes // tok_dev
+    sub = lax.broadcasted_iota(jnp.int32, (tok_dev, lanes), 0)
+    lane = lax.broadcasted_iota(jnp.int32, (tok_dev, lanes), 1)
+    tok = lane - tok_dev * lax.rem(me, per_row)
+    diag = tok == sub
+    e_sub = [ids[:, k:k + 1] for k in range(2)]
+    p_sub = [jnp.sum(jnp.where(lane == e, probs, 0.0), axis=1, keepdims=True) for e in e_sub]
+    total = p_sub[0] + p_sub[1]
+    to_lanes = lambda col: jnp.sum(jnp.where(diag, col, 0.0), axis=0, keepdims=True)
+    e_subf = [e.astype(jnp.float32) for e in e_sub]
+    e_lane = [to_lanes(e) for e in e_subf]
+    valid = jnp.sum(jnp.where(diag, 1.0, 0.0), axis=0, keepdims=True)
+    base = (tok_dev * me).astype(jnp.float32)
+    dests, gates = [], []
+    for k in range(2):
+        same = ((e_subf[0] == e_lane[k]) | (e_subf[1] == e_lane[k])) & (sub < tok)
+        slot = jnp.sum(jnp.where(same, 1.0, 0.0), axis=0, keepdims=True)
+        dests.append(valid * (e_lane[k] * float(seq) + base + slot))
+        gates.append(to_lanes(p_sub[k] / total))
+    row = lax.broadcasted_iota(jnp.int32, (table_rows, lanes), 0)
+    mine = lax.div(me, per_row)
+    n_rows = table_rows // 4
+    table = jnp.zeros((table_rows, lanes), jnp.float32)
+    for n, vec in enumerate(dests + gates):
+        table = jnp.where(row == n * n_rows + mine, vec, table)
+    return table
+
+
+def build_kernel(n_chips, h_ref, table_ref, out_ref, hid_ref):
+    step = pl.program_id(0)
+    me = lax.axis_index('sp')
+    experts_dev = pl.num_programs(0)
+    n_cols, tok_chip, cols = h_ref.shape[1], h_ref.shape[2], h_ref.shape[3]
+    seq = n_chips * tok_chip
+    n_rows = table_ref.shape[0] // 4
+    table = table_ref[...]
+    spread = lambda n: jnp.concatenate([table[n * n_rows + r:n * n_rows + r + 1, :] for r in range(n_rows)], axis=1)
+    dest = [spread(0), spread(1)]
+    gate = [spread(2), spread(3)]
+    expert = me * experts_dev + step
+
+    @pl.when(step == 0)
+    def _():
+        tok_dev = hid_ref.shape[0]
+        per_chip = tok_chip // tok_dev
+        chip = lax.div(me, per_chip)
+        first = pl.multiple_of(lax.rem(me, per_chip) * tok_dev, tok_dev)
+        for n in range(n_cols):
+            hid_ref[:, n * cols:(n + 1) * cols] = h_ref[chip, n, pl.ds(first, tok_dev), :]
+
+    row = (lax.broadcasted_iota(jnp.int32, (seq, seq), 0) + expert * seq).astype(jnp.float32)
+    hit = [dest[0] == row, dest[1] == row]
+    gate_row = jnp.sum(jnp.where(hit[0], gate[0], 0.0) + jnp.where(hit[1], gate[1], 0.0), axis=1, keepdims=True)
+    picks = jnp.where(hit[0] | hit[1], 1.0, 0.0)
+    any_row = jnp.sum(picks) > 0.0
+
+    @pl.when(any_row)
+    def _():
+        pick = picks.astype(jnp.bfloat16)
+        for n in range(n_cols):
+            rows = h_ref[:, n].reshape(seq, cols)
+            got = jnp.dot(pick, rows, preferred_element_type=jnp.float32)
+            out_ref[0, :, n * cols:(n + 1) * cols] = (got * gate_row).astype(jnp.bfloat16)
+
+    @pl.when(jnp.logical_not(any_row))
+    def _():
+        out_ref[...] = jnp.zeros_like(out_ref)
+
+
+def build_buffers(h_all, table, tok_dev, experts_dev):
+    n_chips, n_cols, tok_chip, cols = h_all.shape
+    seq, width = n_chips * tok_chip, n_cols * cols
+    return pl.pallas_call(
+        functools.partial(build_kernel, n_chips),
+        name='build_buffers',
+        grid=(experts_dev,),
+        in_specs=[pl.BlockSpec(h_all.shape, lambda e: (0, 0, 0, 0)), pl.BlockSpec(table.shape, lambda e: (0, 0))],
+        out_specs=[pl.BlockSpec((1, seq, width), lambda e: (e, 0, 0)), pl.BlockSpec((tok_dev, width), lambda e: (0, 0))],
+        out_shape=[jax.ShapeDtypeStruct((experts_dev, seq, width), jnp.bfloat16), jax.ShapeDtypeStruct((tok_dev, width), jnp.bfloat16)],
+        compiler_params=pltpu.CompilerParams(vmem_limit_bytes=32 * 1024 * 1024),
+        cost_estimate=pl.CostEstimate(flops=2 * experts_dev * seq * seq * width, bytes_accessed=2 * experts_dev * seq * width, transcendentals=0),
+    )(h_all, table)
 
 
 def solution(mesh):
@@ -27,7 +105,7 @@
     buf_spec = P(('dp', 'sp'), None, None)
 
     def device_step(x_loc, w_q, w_k, w_v, w_o, ids_loc, probs_loc):
-        tok_dev = x_loc.shape[0]
+        tok_dev, width = x_loc.shape
         seq_len = tok_dev * group
         n_heads = w_q.shape[1] // HEAD_DIM
         kv_heads = w_k.shape[1] // HEAD_DIM
@@ -52,8 +130,12 @@
         attn_loc = lax.all_to_all(attn_seq, 'sp', 0, 1, tiled=True).reshape(tok_dev, n_heads * HEAD_DIM)
         out_proj = jnp.dot(attn_loc, w_o, preferred_element_type=jnp.float32)
         hidden_out = (x_loc.astype(jnp.float32) + out_proj).astype(jnp.bfloat16)
-        send_buf = route_rows(hidden_out, ids_loc, probs_loc)
-        recv_buf = lax.all_to_all(send_buf, 'sp', 0, 1, tiled=True)
-        return hidden_out, recv_buf
+        experts_dev = probs_loc.shape[1] // group
+        table = route_table(lax.axis_index('sp'), ids_loc, probs_loc, seq_len, 4 * seq_len // probs_loc.shape[1])
+        table = jnp.sum(lax.all_gather(table, 'sp', axis=0), axis=0)
+        h_all = lax.all_gather(hidden_out, 'sp', axis=0, tiled=True)
+        h_all = h_all.reshape(group // 2, 2 * tok_dev, width // COLS, COLS).transpose(0, 2, 1, 3)
+        buf, hid = build_buffers(h_all, table, tok_dev, experts_dev)
+        return hid, buf
 
     return jax.shard_map(device_step, mesh=mesh, in_specs=(row_spec, P(), P(), P(), P(), row_spec, row_spec), out_specs=(row_spec, buf_spec), check_vma=False)

time: 535 us -> 203 us (0.38)
  blocking collectives: 366 us -> 34.7 us
  local copies, waits for them, and re-layouts: 27.7 us -> 6.08 us
  between operations: 0.82 us -> 14.3 us
  Pallas kernels: 0 us -> 9.6 us
    all_to_all x1, blocking collectives: 366 us -> 20 us  [device_step(): lax.all_to_all(attn_seq, 'sp', 0, 1, tiled=True)]
    all_gather x0 -> x1, waiting for transfers between devices: none -> 18.7 us  [device_step(): h_all = lax.all_gather(hidden_out, 'sp', axis=0, tiled=True)]
    all_gather x0 -> x1, blocking collectives: none -> 14.7 us  [device_step(): table = jnp.sum(lax.all_gather(table, 'sp', axis=0), axis=0)]
    all_to_all x1 -> x0, waiting for transfers between devices: 14.4 us -> none  [device_step(): lax.all_to_all(attn_seq, 'sp', 0, 1, tiled=True)]
    pallas_call x0 -> x1, Pallas kernels: none -> 9.6 us  [build_buffers(): pl.pallas_call(functools.partial(build_kernel, n_chips), name='build_buff...]
    scatter x1 -> x0, local copies, waits for them, and re-layouts: 9 us -> none  [route_rows(): return send_buf.at[expert_ids, slot_rank].set(gated, unique_indices=True)]
    all_to_all x1 -> x0, local copies, waits for them, and re-layouts: 6.52 us -> none  [device_step(): recv_buf = lax.all_to_all(send_buf, 'sp', 0, 1, tiled=True)]
    broadcast_in_dim x1 -> x0, local copies, waits for them, and re-layouts: 6.1 us -> none  [route_rows(): send_buf = jnp.zeros((experts, tok_dev, width), jnp.bfloat16)]
  transfers between devices with their start and end apart: 4 -> 4, of which waited for: 4 -> 4; matrix products, arithmetic and copies ran while one was open for 2% -> 5% of each run, Pallas kernels for 0% -> 0%
where the time goes in v1:
time: 203 us
  matrix products  81.9 us (40%)
  waiting for transfers between devices  37.3 us (18%)
  blocking collectives  34.7 us (17%)
  starting transfers between devices  19 us (9%)
  between operations  14.3 us (7%)
  Pallas kernels  9.6 us (5%)
  local copies, waits for them, and re-layouts  6.08 us (3%)
    dot_general x1, matrix products, device_step(): jnp.dot(x_loc, w_q, preferred_element_type=jnp.float32).astype(jnp.bfloat16)  38 us
    dot_general x1, matrix products, device_step(): out_proj = jnp.dot(attn_loc, w_o, preferred_element_type=jnp.float32)  33.9 us
    all_to_all x1, blocking collectives, device_step(): lax.all_to_all(attn_seq, 'sp', 0, 1, tiled=True)  20 us
    all_gather x1, waiting for transfers between devices, device_step(): h_all = lax.all_gather(hidden_out, 'sp', axis=0, tiled=True)  18.7 us
    all_gather x1, blocking collectives, device_step(): table = jnp.sum(lax.all_gather(table, 'sp', axis=0), axis=0)  14.7 us
    all_to_all x1, starting transfers between devices, device_step(): q_seq = lax.all_to_all(q_loc, 'sp', 1, 0, tiled=True)  10.7 us
    pallas_call x1, Pallas kernels, build_buffers(): pl.pallas_call(functools.partial(build_kernel, n_chips), name='build_buff...  9.6 us
    all_to_all x1, waiting for transfers between devices, device_step(): q_seq = lax.all_to_all(q_loc, 'sp', 1, 0, tiled=True)  9.52 us
  transfers between devices with their start and end apart: 4, of which 4 were waited for; matrix products, arithmetic and copies ran while one was open for 5% of the time, Pallas kernels for 0%

profile of v1, /device:TPU:21, one launch (start us, length us, event | category | flops | bytes accessed | tf_op | source)
XLA Modules:
  0.0 203.5 jit_solution(9170516940325356482)
XLA Ops:
  7.2 0.0 copy-start
  7.2 38.0 %fusion.3 = bf16[2,96,8,128]{3,2,1,0:T(8,128)(2,1)S(1)} fusion(bf16[16,4096]{1,0:T(8,128)(2,1)} %param.7, bf16[4096,12288]{1,0:T(8,128)(2,1)} %param.8), kind=kOutput, calls=%fused_computation.10 | convolution fusion | flops 1610809344 | bytes 101187584 | tf_op jit(solution)/shard_map/dot_general | solution.py:115
  45.2 0.8 copy.45
  46.0 10.7 %all-to-all-start.2 = ((bf16[16,96,128]{2,0,1:T(8,128)(2,1)}), bf16[16,96,128]{2,0,1:T(8,128)(2,1)S(1)}, u32[]{:S(2)}, u32[]{:S(2)}) async-start(bf16[16,96,128]{2,0,1:T(8,128)(2,1)} %bitcast.73), calls=%async_computation.2 | async-start | bytes 786432 | tf_op jit(solution)/shard_map/all_to_all | solution.py:120
  56.7 0.0 copy-done
  56.7 4.6 %fusion.5 = bf16[2,8,8,128]{3,2,1,0:T(8,128)(2,1)S(1)} fusion(bf16[16,4096]{1,0:T(8,128)(2,1)S(1)} %copy-done, bf16[4096,1024]{1,0:T(8,128)(2,1)} %param.9), kind=kOutput, calls=%fused_computation.14 | convolution fusion | flops 134234112 | bytes 8552448 | tf_op jit(solution)/shard_map/dot_general | solution.py:116
  61.3 9.5 %all-to-all-done.2 = bf16[16,96,128]{2,0,1:T(8,128)(2,1)S(1)} async-done(((bf16[16,96,128]{2,0,1:T(8,128)(2,1)}), bf16[16,96,128]{2,0,1:T(8,128)(2,1)S(1)}, u32[]{:S(2)}, u32[]{:S(2)}) %all-to-all-start.2) | async-done | bytes 393248 | tf_op jit(solution)/shard_map/all_to_all | solution.py:120
  70.9 0.6 broadcast_in_dim.98
  71.5 3.7 %all-to-all-start.1 = ((bf16[16,16,128]{2,0,1:T(8,128)(2,1)}), bf16[16,16,128]{2,0,1:T(8,128)(2,1)S(1)}, u32[]{:S(2)}, u32[]{:S(2)}) async-start(bf16[16,16,128]{2,0,1:T(8,128)(2,1)} %bitcast.5), calls=%async_computation.1 | async-start | bytes 131072 | tf_op jit(solution)/shard_map/all_to_all | solution.py:121
  75.2 4.6 %fusion.4 = bf16[2,8,8,128]{3,2,1,0:T(8,128)(2,1)S(1)} fusion(bf16[16,4096]{1,0:T(8,128)(2,1)S(1)} %copy-done, bf16[4096,1024]{1,0:T(8,128)(2,1)} %param.10), kind=kOutput, calls=%fused_computation.13 | convolution fusion | flops 134234112 | bytes 8552448 | tf_op jit(solution)/shard_map/dot_general | solution.py:117
  79.8 2.3 %all-to-all-done.1 = bf16[16,16,128]{2,0,1:T(8,128)(2,1)S(1)} async-done(((bf16[16,16,128]{2,0,1:T(8,128)(2,1)}), bf16[16,16,128]{2,0,1:T(8,128)(2,1)S(1)}, u32[]{:S(2)}, u32[]{:S(2)}) %all-to-all-start.1) | async-done | bytes 65568 | tf_op jit(solution)/shard_map/all_to_all | solution.py:121
  82.1 0.6 broadcast_in_dim.96
  82.8 4.5 %all-to-all-start = ((bf16[16,16,128]{2,0,1:T(8,128)(2,1)}), bf16[16,16,128]{2,0,1:T(8,128)(2,1)S(1)}, u32[]{:S(2)}, u32[]{:S(2)}) async-start(bf16[16,16,128]{2,0,1:T(8,128)(2,1)} %bitcast), calls=%async_computation | async-start | bytes 131072 | tf_op jit(solution)/shard_map/all_to_all | solution.py:122
  87.3 0.1 all-gather.2.cloned.1.call-start
  87.4 0.4 fusion.9
  87.8 0.2 fusion.1
  88.0 6.7 %all-to-all-done = bf16[16,16,128]{2,0,1:T(8,128)(2,1)S(1)} async-done(((bf16[16,16,128]{2,0,1:T(8,128)(2,1)}), bf16[16,16,128]{2,0,1:T(8,128)(2,1)S(1)}, u32[]{:S(2)}, u32[]{:S(2)}) %all-to-all-start) | async-done | bytes 65568 | tf_op jit(solution)/shard_map/all_to_all | solution.py:122
  94.7 0.4 fusion.2
  95.1 0.3 copy.28
  95.5 20.0 %all_to_all.60 = bf16[256,6,128]{2,1,0:T(8,128)(2,1)S(1)} all-to-all(bf16[256,6,128]{2,1,0:T(8,128)(2,1)S(1)} %copy.28), channel_id=1, replica_groups=mesh['dp'=4,'sp'=16] {'sp'}, dimensions={0} | all-to-all | bytes 786432 | tf_op jit(solution)/shard_map/all_to_all | solution.py:130
  115.5 0.1 copy.30
  115.6 0.4 reshape.277
  116.0 0.0 copy-start.2
  116.0 0.0 copy-start.1
  116.1 33.9 %fusion = bf16[16,4096]{1,0:T(8,128)(2,1)} fusion(bf16[16,12288]{1,0:T(8,128)(2,1)S(1)} %reshape.277, bf16[12288,4096]{1,0:T(8,128)(2,1)} %param.11, bf16[16,4096]{1,0:T(8,128)(2,1)S(1)} %copy-done), kind=kOutput, calls=%fused_computation.2 | convolution fusion | flops 1610809344 | bytes 101318656 | tf_op jit(solution)/shard_map/dot_general | solution.py:131
  150.0 0.1 all-gather.2.cloned.1.call-update
  150.1 0.0 copy-done.2
  150.1 0.0 copy-done.1
  150.1 0.2 select_reduce_fusion.3
  150.4 0.1 select_reduce_fusion.2
  150.5 0.1 select_select_fusion
  150.5 14.7 %all_gather.8 = f32[16,8,128]{2,1,0:T(8,128)S(1)} all-gather(f32[1,8,128]{2,1,0:T(8,128)S(1)} %select_select_fusion), channel_id=1, replica_groups=mesh['dp'=4,'sp'=16] {'sp'}, dimensions={0}, use_global_device_ids=true | all-gather | bytes 69632 | tf_op jit(solution)/shard_map/all_gather | solution.py:135
  165.2 18.7 %all-gather.2.cloned.1.call-done = bf16[256,4096]{1,0:T(8,128)(2,1)} async-done(((bf16[16,4096]{1,0:T(8,128)(2,1)}), bf16[256,4096]{1,0:T(8,128)(2,1)}) %all-gather.2.cloned.1.call-update) | async-done | bytes 2097168 | tf_op jit(solution)/shard_map/all_gather | solution.py:136
  184.0 2.2 %copy.39 = bf16[32,8,16,256]{3,2,1,0:T(8,128)(2,1)S(1)} copy(bf16[32,8,16,256]{3,1,2,0:T(8,128)(2,1)} %bitcast.78) | data formatting | bytes 4194304
  186.2 0.8 copy.44
  187.0 9.6 %build_buffers.1 = (bf16[8,256,4096]{2,1,0:T(8,128)(2,1)}, bf16[16,4096]{1,0:T(8,128)(2,1)}) custom-call(bf16[8,16,32,256]{3,2,1,0:T(8,128)(2,1)S(1)} %bitcast.76, f32[8,128]{1,0:T(8,128)S(1)} %reduce_sum.109.table_ref), custom_call_target="tpu_custom_call" | custom-call | flops 4294967296 | bytes 16777216 | tf_op jit(solution)/shard_map/build_buffers/pallas_call | solution.py:90
  (11 shorter events, 0.1 us)
Async XLA Ops:
  7.2 49.6 %copy-start = (bf16[16,4096]{1,0:T(8,128)(2,1)S(1)}, bf16[16,4096]{1,0:T(8,128)(2,1)}, u32[]{:S(2)}) copy-start(bf16[16,4096]{1,0:T(8,128)(2,1)} %param.7) | copy-start | bytes 393220
  46.0 24.8 %all-to-all-start.2 = ((bf16[16,96,128]{2,0,1:T(8,128)(2,1)}), bf16[16,96,128]{2,0,1:T(8,128)(2,1)S(1)}, u32[]{:S(2)}, u32[]{:S(2)}) async-start(bf16[16,96,128]{2,0,1:T(8,128)(2,1)} %bitcast.73), calls=%async_computation.2 | async-start | bytes 786432 | tf_op jit(solution)/shard_map/all_to_all | solution.py:120
  71.5 10.6 %all-to-all-start.1 = ((bf16[16,16,128]{2,0,1:T(8,128)(2,1)}), bf16[16,16,128]{2,0,1:T(8,128)(2,1)S(1)}, u32[]{:S(2)}, u32[]{:S(2)}) async-start(bf16[16,16,128]{2,0,1:T(8,128)(2,1)} %bitcast.5), calls=%async_computation.1 | async-start | bytes 131072 | tf_op jit(solution)/shard_map/all_to_all | solution.py:121
  82.8 11.9 %all-to-all-start = ((bf16[16,16,128]{2,0,1:T(8,128)(2,1)}), bf16[16,16,128]{2,0,1:T(8,128)(2,1)S(1)}, u32[]{:S(2)}, u32[]{:S(2)}) async-start(bf16[16,16,128]{2,0,1:T(8,128)(2,1)} %bitcast), calls=%async_computation | async-start | bytes 131072 | tf_op jit(solution)/shard_map/all_to_all | solution.py:122
  87.3 96.7 %all-gather.2.cloned.1.call-start = ((), (), s32[]{:S(2)}) async-start(), calls=%async_computation.4 | async-start | bytes 2228224 | tf_op jit(solution)/shard_map/all_gather | solution.py:136
  116.0 34.1 %copy-start.2 = (s32[16,2]{0,1:T(2,128)S(1)}, s32[16,2]{0,1:T(2,128)}, u32[]{:S(2)}) copy-start(s32[16,2]{0,1:T(2,128)} %param.12) | copy-start | bytes 388
  116.0 34.1 %copy-start.1 = (f32[16,128]{1,0:T(8,128)S(1)}, f32[16,128]{1,0:T(8,128)}, u32[]{:S(2)}) copy-start(f32[16,128]{1,0:T(8,128)} %param.13) | copy-start | bytes 24580
Sparse Core Ops, SparseCore 0:
  150.2 33.7 all-gather.1

commit v2 on v1

--- a/solution.py
+++ b/solution.py
@@ -99,43 +99,312 @@
     )(h_all, table)
 
 
+MESH = pl.DeviceIdType.MESH
+ROWS = 2048
+LAG = 2
+
+
+def block_kernel(group, x_hbm, wq, wk, wv, wo, ids, probs, h_out, table_out, wbuf, x_buf, kv, q_buf, o_buf, h_all, tab_pair, tabs,
+                 w_sem, x_sem, pair_send, pair_recv, kv_send, kv_recv, tab_send, tab_recv, o_send, o_recv,
+                 h_send, h_recv, d_send, d_recv, out_sem):
+    tok_dev, width = x_hbm.shape
+    chips = kv.shape[0]
+    tok_chip = x_buf.shape[0]
+    seq = chips * tok_chip
+    heads_core = q_buf.shape[0]
+    kv_core = kv.shape[3] // HEAD_DIM
+    per_kv = heads_core // kv_core
+    q_core = heads_core * HEAD_DIM
+    out_core = width // 2
+    me = lax.axis_index('sp')
+    chip, core = lax.div(me, 2), lax.rem(me, 2)
+    other = 1 - core
+    partner = {'sp': 2 * chip + other}
+    ahead = {'sp': 2 * lax.rem(chip + 1, chips) + core}
+    behind = {'sp': 2 * lax.rem(chip + chips - 1, chips) + core}
+
+    def remote(src, dst, send, recv, device):
+        return pltpu.make_async_remote_copy(src_ref=src, dst_ref=dst, send_sem=send, recv_sem=recv, device_id=device, device_id_type=MESH)
+
+    n_slots = wbuf.shape[0]
+    kv_units = 2 * (kv.shape[3] // COLS) * (width // ROWS)
+    half_units = q_core // ROWS
+    chunk_units = 2 * half_units
+    in_units = width // ROWS
+    q_chunks = q_core // COLS
+    o_chunks = out_core // COLS
+    kv_chunks = kv.shape[3] // COLS
+
+    def load(src, row, col, slot):
+        return pltpu.make_async_copy(src.at[pl.ds(row, ROWS), pl.ds(pl.multiple_of(col, COLS), COLS)], wbuf.at[slot], w_sem.at[slot])
+
+    def wait_unit(slot):
+        load(wk, 0, 0, slot).wait()
+
+    def start_q(n):
+        for r in range(in_units):
+            load(wq, r * ROWS, core * q_core + n * COLS, lax.rem(kv_units + in_units * n + r, n_slots)).start()
+
+    first_o = kv_units + in_units * q_chunks - n_slots
+
+    def start_o(k):
+        j, r = lax.div(k, chunk_units), lax.rem(k, chunk_units)
+        half = jnp.where(r < half_units, core, other)
+        row = pl.multiple_of(half * q_core + lax.rem(r, half_units) * ROWS, ROWS)
+        load(wo, row, core * out_core + j * COLS, first_o + k).start()
+
+    own = pl.ds(pl.multiple_of(core * tok_dev, tok_dev), tok_dev)
+    x_in = pltpu.make_async_copy(x_hbm, x_buf.at[own], x_sem)
+    x_in.start()
+    slot = 0
+    for src in (wk, wv):
+        for n in range(kv_chunks):
+            for r in range(in_units):
+                load(src, r * ROWS, core * kv.shape[3] + n * COLS, slot).start()
+                slot += 1
+    q_first = (n_slots - kv_units) // in_units
+    lax.fori_loop(0, q_first, lambda n, c: (start_q(n), c)[1], 0)
+
+    barrier = pltpu.get_barrier_semaphore()
+    for device in (partner, ahead, behind):
+        pl.semaphore_signal(barrier, inc=1, device_id=device, device_id_type=MESH)
+    tab_pair[0] = route_table(me, ids[...], probs[...], seq, tab_pair.shape[1])
+    x_in.wait()
+    pl.semaphore_wait(barrier, 3)
+
+    x_pair = remote(x_buf.at[own], x_buf.at[own], pair_send.at[0], pair_recv.at[0], partner)
+    t_pair = remote(tab_pair.at[0], tab_pair.at[1], pair_send.at[1], pair_recv.at[1], partner)
+    x_pair.start()
+    t_pair.start()
+    theirs = pl.ds(pl.multiple_of(other * tok_dev, tok_dev), tok_dev)
+    remote(x_buf.at[theirs], x_buf.at[theirs], pair_send.at[0], pair_recv.at[0], partner).wait_recv()
+    t_pair.wait_recv()
+    tabs[chip] = tab_pair[0] + tab_pair[1]
+
+    def project(pair_slot):
+        for r in range(in_units):
+            wait_unit(pair_slot + r)
+        w = wbuf[pl.ds(pair_slot, in_units)].reshape(width, COLS)
+        return jnp.dot(x_buf[...], w, preferred_element_type=jnp.float32).astype(jnp.bfloat16)
+
+    slot = 0
+    for which in range(2):
+        for n in range(kv_chunks):
+            kv[chip, which, :, n * COLS:(n + 1) * COLS] = project(slot)
+            slot += in_units
+
+    for n in range(q_first, q_chunks):
+        start_q(n)
+    early = kv_units - first_o
+    for k in range(early):
+        start_o(k)
+
+    def ring(buf, sends, recvs, s, back):
+        block = lax.rem(chip + s, chips) if back else lax.rem(chip + chips - s, chips)
+        n = 4 * back + s
+        return remote(buf.at[block], buf.at[block], sends.at[n], recvs.at[n], behind if back else ahead)
+
+    def ring_in(buf, sends, recvs, s, back):
+        block = lax.rem(chip + s + 1, chips) if back else lax.rem(chip + chips - s - 1, chips)
+        n = 4 * back + s
+        return remote(buf.at[block], buf.at[block], sends.at[n], recvs.at[n], behind if back else ahead)
+
+    small = ((kv, kv_send, kv_recv), (tabs, tab_send, tab_recv))
+    fwd, bwd = chips // 2, chips // 2 - 1
+    for args in small:
+        ring(*args, 0, 0).start()
+        ring(*args, 0, 1).start()
+
+    heads_chunk = COLS // HEAD_DIM
+
+    def q_step(n, carry):
+        res = project(lax.rem(kv_units + in_units * n, n_slots))
+        for i in range(heads_chunk):
+            q_buf[heads_chunk * n + i] = res[:, i * HEAD_DIM:(i + 1) * HEAD_DIM]
+
+        @pl.when(n < q_first)
+        def _():
+            for r in range(in_units):
+                start_o(early + in_units * n + r)
+        return carry
+
+    part = q_chunks // fwd
+    for s in range(fwd):
+        lax.fori_loop(s * part, (s + 1) * part, q_step, 0)
+        for args in small:
+            ring_in(*args, s, 0).wait_recv()
+            if s + 1 < fwd:
+                ring(*args, s + 1, 0).start()
+            if s < bwd:
+                ring_in(*args, s, 1).wait_recv()
+                if s + 1 < bwd:
+                    ring(*args, s + 1, 1).start()
+
+    rows = per_kv * tok_chip
+    q_pos = tok_chip * chip + lax.rem(lax.broadcasted_iota(jnp.int32, (rows, seq), 0), tok_chip)
+    seen = lax.broadcasted_iota(jnp.int32, (rows, seq), 1) <= q_pos
+    o_copies = []
+    for g in range(kv_core):
+        lanes = slice(g * HEAD_DIM, (g + 1) * HEAD_DIM)
+        qg = q_buf[g * per_kv:(g + 1) * per_kv].reshape(rows, HEAD_DIM)
+        kg = kv[:, 0, :, lanes].reshape(seq, HEAD_DIM)
+        vg = kv[:, 1, :, lanes].reshape(seq, HEAD_DIM)
+        s = lax.dot_general(qg, kg, (((1,), (1,)), ((), ())), preferred_element_type=jnp.float32) * SCORE_SCALE
+        s = jnp.where(seen, s, -1e30)
+        p = jnp.exp(s - jnp.max(s, axis=1, keepdims=True))
+        p = (p / jnp.sum(p, axis=1, keepdims=True)).astype(jnp.bfloat16)
+        o = jnp.dot(p, vg, preferred_element_type=jnp.float32).astype(jnp.bfloat16)
+        for h in range(per_kv):
+            at = (g * per_kv + h) * HEAD_DIM
+            o_buf[0, :, at:at + HEAD_DIM] = o[h * tok_chip:(h + 1) * tok_chip]
+        span = pl.ds(g * per_kv * HEAD_DIM, per_kv * HEAD_DIM)
+        copy = remote(o_buf.at[0, :, span], o_buf.at[1, :, span], o_send.at[g], o_recv.at[g], partner)
+        copy.start()
+        o_copies.append(copy)
+
+    def h_piece(block, j, s, back):
+        piece = h_all.at[block, core * o_chunks + j]
+        if s == fwd - 1:
+            piece = piece.at[pl.ds(back * tok_dev, tok_dev)]
+        return piece
+
+    def h_ring(j, s, back):
+        block = lax.rem(chip + s, chips) if back else lax.rem(chip + chips - s, chips)
+        piece = h_piece(block, j, s, back)
+        return remote(piece, piece, h_send.at[j, 4 * back + s], h_recv.at[j, 4 * back + s], behind if back else ahead)
+
+    def h_ring_in(j, s, back):
+        block = lax.rem(chip + s + 1, chips) if back else lax.rem(chip + chips - s - 1, chips)
+        piece = h_piece(block, j, s, back)
+        return remote(piece, piece, h_send.at[j, 4 * back + s], h_recv.at[j, 4 * back + s], behind if back else ahead)
+
+    def h_pair(j):
+        cols = h_all.at[:, core * o_chunks + j]
+        return remote(cols, cols, d_send.at[j], d_recv.at[j], partner)
+
+    def h_pair_in(j):
+        cols = h_all.at[:, other * o_chunks + j]
+        return remote(cols, cols, d_send.at[j], d_recv.at[j], partner)
+
+    def h_hop(j, s):
+        for back in range(2):
+            h_ring_in(j, s, back).wait_recv()
+            if s + 1 < fwd:
+                h_ring(j, s + 1, back).start()
+        if s + 1 == fwd:
+            h_pair(j).start()
+
+    def o_step(j, carry):
+        at = first_o + chunk_units * j
+        for r in range(half_units):
+            wait_unit(at + r)
+        acc = jnp.dot(o_buf[0], wbuf[pl.ds(at, half_units)].reshape(q_core, COLS), preferred_element_type=jnp.float32)
+
+        @pl.when(j == 0)
+        def _():
+            for copy in o_copies:
+                copy.wait_recv()
+        for r in range(half_units):
+            wait_unit(at + half_units + r)
+        acc += jnp.dot(o_buf[1], wbuf[pl.ds(at + half_units, half_units)].reshape(q_core, COLS), preferred_element_type=jnp.float32)
+        x_cols = x_buf[:, pl.ds(pl.multiple_of(core * out_core + j * COLS, COLS), COLS)]
+        h_all[chip, core * o_chunks + j] = (x_cols.astype(jnp.float32) + acc).astype(jnp.bfloat16)
+        for back in range(2):
+            h_ring(j, 0, back).start()
+        for s in range(fwd):
+            late = LAG * (s + 1)
+            if late < o_chunks:
+                @pl.when(j >= late)
+                def _(s=s, late=late):
+                    h_hop(j - late, s)
+        return carry
+
+    lax.fori_loop(0, o_chunks, o_step, 0)
+
+    def put(j, half):
+        cols = half * o_chunks + j
+        return pltpu.make_async_copy(h_all.at[:, cols], h_out.at[:, cols], out_sem.at[j, half])
+
+    done = []
+    for t in range(o_chunks, o_chunks + LAG * fwd):
+        for s in reversed(range(fwd)):
+            j = t - LAG * (s + 1)
+            if 0 <= j < o_chunks:
+                h_hop(j, s)
+                if s + 1 == fwd:
+                    done.append(j)
+    for j in done:
+        put(j, core).start()
+    for j in done:
+        h_pair_in(j).wait_recv()
+        put(j, other).start()
+    table_out[...] = jnp.sum(tabs[...], axis=0)
+
+    x_pair.wait_send()
+    t_pair.wait_send()
+    for args in small:
+        for back, hops in ((0, fwd), (1, bwd)):
+            for s in range(hops):
+                ring(*args, s, back).wait_send()
+    for copy in o_copies:
+        copy.wait_send()
+    for j in range(o_chunks):
+        for s in range(fwd):
+            for back in range(2):
+                h_ring(j, s, back).wait_send()
+        h_pair(j).wait_send()
+        put(j, core).wait()
+        put(j, other).wait()
+
+
+def attend(x_loc, w_q, w_k, w_v, w_o, ids, probs, group):
+    tok_dev, width = x_loc.shape
+    chips = group // 2
+    tok_chip = 2 * tok_dev
+    heads_core = w_q.shape[1] // HEAD_DIM // 2
+    kv_width = w_k.shape[1] // 2
+    q_core = heads_core * HEAD_DIM
+    lanes = probs.shape[1]
+    table_rows = 4 * chips * tok_chip // lanes
+    o_chunks = width // 2 // COLS
+    kv_core = kv_width // HEAD_DIM
+    kv_units = 2 * kv_width // COLS * (width // ROWS)
+    units = kv_units + (q_core // COLS) * (width // ROWS) + o_chunks * 2 * q_core // ROWS
+    n_slots = units // 2
+    bf16, f32 = jnp.bfloat16, jnp.float32
+    dma = pltpu.SemaphoreType.DMA
+    anywhere = pl.BlockSpec(memory_space=pl.ANY)
+    in_vmem = pl.BlockSpec(memory_space=pltpu.VMEM)
+    return pl.pallas_call(
+        functools.partial(block_kernel, group),
+        name='attend',
+        in_specs=[anywhere] * 5 + [in_vmem] * 2,
+        out_specs=[anywhere, in_vmem],
+        out_shape=[jax.ShapeDtypeStruct((chips, width // COLS, tok_chip, COLS), bf16), jax.ShapeDtypeStruct((table_rows, lanes), f32)],
+        scratch_shapes=[
+            pltpu.VMEM((n_slots, ROWS, COLS), bf16),
+            pltpu.VMEM((tok_chip, width), bf16),
+            pltpu.VMEM((chips, 2, tok_chip, kv_width), bf16),
+            pltpu.VMEM((heads_core, tok_chip, HEAD_DIM), bf16),
+            pltpu.VMEM((2, tok_chip, q_core), bf16),
+            pltpu.VMEM((chips, width // COLS, tok_chip, COLS), bf16),
+            pltpu.VMEM((2, table_rows, lanes), f32),
+            pltpu.VMEM((chips, table_rows, lanes), f32),
+            dma((n_slots,)), dma, dma((2,)), dma((2,)), dma((8,)), dma((8,)), dma((8,)), dma((8,)), dma((kv_core,)), dma((kv_core,)),
+            dma((o_chunks, 8)), dma((o_chunks, 8)), dma((o_chunks,)), dma((o_chunks,)), dma((o_chunks, 2)),
+        ],
+        compiler_params=pltpu.CompilerParams(collective_id=0, has_side_effects=True, vmem_limit_bytes=65_000_000),
+    )(x_loc, w_q, w_k, w_v, w_o, ids, probs)
+
+
 def solution(mesh):
     group = mesh.shape['sp']
     row_spec = P(('dp', 'sp'), None)
     buf_spec = P(('dp', 'sp'), None, None)
 
     def device_step(x_loc, w_q, w_k, w_v, w_o, ids_loc, probs_loc):
-        tok_dev, width = x_loc.shape
-        seq_len = tok_dev * group
-        n_heads = w_q.shape[1] // HEAD_DIM
-        kv_heads = w_k.shape[1] // HEAD_DIM
-        kv_copies = max(1, group // kv_heads)
-        head_dev = n_heads // group
-        kv_dev = kv_heads * kv_copies // group
-        q_loc = jnp.dot(x_loc, w_q, preferred_element_type=jnp.float32).astype(jnp.bfloat16).reshape(tok_dev, n_heads, HEAD_DIM)
-        k_loc = jnp.dot(x_loc, w_k, preferred_element_type=jnp.float32).astype(jnp.bfloat16).reshape(tok_dev, kv_heads, HEAD_DIM)
-        v_loc = jnp.dot(x_loc, w_v, preferred_element_type=jnp.float32).astype(jnp.bfloat16).reshape(tok_dev, kv_heads, HEAD_DIM)
-        k_loc = jnp.repeat(k_loc, kv_copies, axis=1)
-        v_loc = jnp.repeat(v_loc, kv_copies, axis=1)
-        q_seq = lax.all_to_all(q_loc, 'sp', 1, 0, tiled=True)
-        k_seq = lax.all_to_all(k_loc, 'sp', 1, 0, tiled=True)
-        v_seq = lax.all_to_all(v_loc, 'sp', 1, 0, tiled=True)
-        q_grp = q_seq.reshape(seq_len, kv_dev, head_dev // kv_dev, HEAD_DIM)
-        scores = jnp.einsum('qgmd,kgd->gmqk', q_grp, k_seq, preferred_element_type=jnp.float32) * SCORE_SCALE
-        positions = jnp.arange(seq_len)
-        causal = positions[:, None] >= positions[None, :]
-        weights = jax.nn.softmax(jnp.where(causal, scores, -1e30), axis=-1).astype(jnp.bfloat16)
-        attn_seq = jnp.einsum('gmqk,kgd->qgmd', weights, v_seq, preferred_element_type=jnp.float32).astype(jnp.bfloat16)
-        attn_seq = attn_seq.reshape(seq_len, head_dev, HEAD_DIM)
-        attn_loc = lax.all_to_all(attn_seq, 'sp', 0, 1, tiled=True).reshape(tok_dev, n_heads * HEAD_DIM)
-        out_proj = jnp.dot(attn_loc, w_o, preferred_element_type=jnp.float32)
-        hidden_out = (x_loc.astype(jnp.float32) + out_proj).astype(jnp.bfloat16)
-        experts_dev = probs_loc.shape[1] // group
-        table = route_table(lax.axis_index('sp'), ids_loc, probs_loc, seq_len, 4 * seq_len // probs_loc.shape[1])
-        table = jnp.sum(lax.all_gather(table, 'sp', axis=0), axis=0)
-        h_all = lax.all_gather(hidden_out, 'sp', axis=0, tiled=True)
-        h_all = h_all.reshape(group // 2, 2 * tok_dev, width // COLS, COLS).transpose(0, 2, 1, 3)
-        buf, hid = build_buffers(h_all, table, tok_dev, experts_dev)
+        h_all, table = attend(x_loc, w_q, w_k, w_v, w_o, ids_loc, probs_loc, group)
+        buf, hid = build_buffers(h_all, table, x_loc.shape[0], probs_loc.shape[1] // group)
         return hid, buf
 
     return jax.shard_map(device_step, mesh=mesh, in_specs=(row_spec, P(), P(), P(), P(), row_spec, row_spec), out_specs=(row_spec, buf_spec), check_vma=False)

time: 203 us -> 77.3 us (0.38)
  matrix products: 81.9 us -> 0 us
  Pallas kernels: 9.6 us -> 73.2 us
  waiting for transfers between devices: 37.3 us -> 0 us
  blocking collectives: 34.7 us -> 0 us
  starting transfers between devices: 19 us -> 0 us
  between operations: 14.3 us -> 0.65 us
  local copies, waits for them, and re-layouts: 6.08 us -> 3.62 us
    dot_general x6 -> x0, matrix products: 81.9 us -> none  [the longest x1 38 us: device_step(): jnp.dot(x_loc, w_q, preferred_element_type=jnp.float32).astype(jnp.bfloat16)]
    pallas_call x0 -> x1, Pallas kernels: none -> 63.1 us  [attend(): pl.pallas_call(functools.partial(block_kernel, group), name='attend', in_...]
    all_to_all x1 -> x0, blocking collectives: 20 us -> none  [device_step(): lax.all_to_all(attn_seq, 'sp', 0, 1, tiled=True)]
    all_to_all x3 -> x0, starting transfers between devices: 18.9 us -> none  [the longest x1 10.7 us: device_step(): q_seq = lax.all_to_all(q_loc, 'sp', 1, 0, tiled=True)]
    all_gather x1 -> x0, waiting for transfers between devices: 18.7 us -> none  [device_step(): h_all = lax.all_gather(hidden_out, 'sp', axis=0, tiled=True)]
    all_to_all x3 -> x0, waiting for transfers between devices: 18.5 us -> none  [the longest x1 9.52 us: device_step(): q_seq = lax.all_to_all(q_loc, 'sp', 1, 0, tiled=True)]
    all_gather x1 -> x0, blocking collectives: 14.7 us -> none  [device_step(): table = jnp.sum(lax.all_gather(table, 'sp', axis=0), axis=0)]
    reshape x6 -> x0, local copies, waits for them, and re-layouts: 2.4 us -> none  [the longest x1 0.82 us: device_step(): jnp.dot(x_loc, w_q, preferred_element_type=jnp.float32).astype(jnp.bfloat16)]
  transfers between devices with their start and end apart: 4 -> 0, of which waited for: 4 -> 0; matrix products, arithmetic and copies ran while one was open for 5% -> 0% of each run, Pallas kernels for 0% -> 0%
where the time goes in v2:
time: 77.3 us; the launch traced here: 77.5 us
  Pallas kernels  73.2 us (95%)
  local copies, waits for them, and re-layouts  3.62 us (5%)
    pallas_call x1, Pallas kernels, attend(): pl.pallas_call(functools.partial(block_kernel, group), name='attend', in_...  63.1 us
    pallas_call x1, Pallas kernels, build_buffers(): pl.pallas_call(functools.partial(build_kernel, n_chips), name='build_buff...  10.1 us
    unnamed x5, local copies, waits for them, and re-layouts  3.62 us

profile of v2, /device:TPU:21, one launch (start us, length us, event | category | flops | bytes accessed | tf_op | source)
XLA Modules:
  0.0 77.5 jit_solution(12389586786926057787)
XLA Ops:
  0.6 1.4 %copy.9.ids = s32[16,2]{1,0:T(8,128)} copy(s32[16,2]{0,1:T(2,128)} %param.12) | data formatting | bytes 256 | tf_op args[5]
  2.0 63.1 %attend.1 = (bf16[8,16,32,256]{3,2,1,0:T(8,128)(2,1)}, f32[8,128]{1,0:T(8,128)}) custom-call(bf16[16,4096]{1,0:T(8,128)(2,1)} %x_hbm.1, bf16[4096,12288]{1,0:T(8,128)(2,1)} %wq.1, bf16[4096,1024]{1,0:T(8,128)(2,1)} %wk.1, bf16[4096,1024]{1,0:T(8,128)(2,1)} %wv.1, bf16[12288,4096]{1,0:T(8,128)(2,1)} %wo.1, s32[16,2]{1,0:T(8,128)} %copy.9.ids, f32[16,128]{1,0:T(8,128)} %probs.1), custom_call_target="tpu_custom_call" | custom-call | tf_op jit(solution)/shard_map/attend/pallas_call | solution.py:378
  65.1 0.0 copy-start
  65.1 1.6 %copy-done = bf16[8,16,32,256]{3,2,1,0:T(8,128)(2,1)S(1)} copy-done((bf16[8,16,32,256]{3,2,1,0:T(8,128)(2,1)S(1)}, bf16[8,16,32,256]{3,2,1,0:T(8,128)(2,1)}, u32[]{:S(2)}) %copy-start) | copy-done | bytes 2097176
  66.7 0.0 copy-start.1
  66.7 0.7 copy-done.1
  67.3 10.1 %build_buffers.1 = (bf16[8,256,4096]{2,1,0:T(8,128)(2,1)}, bf16[16,4096]{1,0:T(8,128)(2,1)}) custom-call(bf16[8,16,32,256]{3,2,1,0:T(8,128)(2,1)S(1)} %copy-done, f32[8,128]{1,0:T(8,128)S(1)} %copy-done.1), custom_call_target="tpu_custom_call" | custom-call | flops 4294967296 | bytes 16777216 | tf_op jit(solution)/shard_map/build_buffers/pallas_call | solution.py:90
Async XLA Ops:
  65.1 1.6 %copy-start = (bf16[8,16,32,256]{3,2,1,0:T(8,128)(2,1)S(1)}, bf16[8,16,32,256]{3,2,1,0:T(8,128)(2,1)}, u32[]{:S(2)}) copy-start(bf16[8,16,32,256]{3,2,1,0:T(8,128)(2,1)} %get-tuple-element.6.h_ref) | copy-start | bytes 6291460
  66.7 0.7 copy-start.1

commit v3 on v2

v3 whole, which is shorter than its diff:
```python
import math
import functools
import jax
import jax.numpy as jnp
from jax import lax
from jax.experimental import pallas as pl
from jax.experimental.pallas import tpu as pltpu
from jax.sharding import PartitionSpec as P

HEAD_DIM = 128
SCORE_SCALE = 1.0 / math.sqrt(HEAD_DIM)
COLS = 256
ROWS = 2048
LAG = 2
CHAIN = 4
GROUP_ROWS = 128
MESH = pl.DeviceIdType.MESH


def route_table(me, ids, probs, seq, table_rows):
    tok_dev, lanes = probs.shape
    per_row = lanes // tok_dev
    sub = lax.broadcasted_iota(jnp.int32, (tok_dev, lanes), 0)
    lane = lax.broadcasted_iota(jnp.int32, (tok_dev, lanes), 1)
    tok = lane - tok_dev * lax.rem(me, per_row)
    diag = tok == sub
    square = lax.broadcasted_iota(jnp.int32, (tok_dev, tok_dev), 0) == lax.broadcasted_iota(jnp.int32, (tok_dev, tok_dev), 1)
    ids = ids.astype(jnp.float32)
    e_sub = [jnp.sum(jnp.where(square, ids[k:k + 1, :], 0.0), axis=1, keepdims=True) for k in range(2)]
    lane_f = lane.astype(jnp.float32)
    p_sub = [jnp.sum(jnp.where(lane_f == e, probs, 0.0), axis=1, keepdims=True) for e in e_sub]
    total = p_sub[0] + p_sub[1]
    to_lanes = lambda col: jnp.sum(jnp.where(diag, col, 0.0), axis=0, keepdims=True)
    e_lane = [to_lanes(e) for e in e_sub]
    valid = jnp.sum(jnp.where(diag, 1.0, 0.0), axis=0, keepdims=True)
    base = (tok_dev * me).astype(jnp.float32)
    dests, gates = [], []
    for k in range(2):
        same = ((e_sub[0] == e_lane[k]) | (e_sub[1] == e_lane[k])) & (sub < tok)
        slot = jnp.sum(jnp.where(same, 1.0, 0.0), axis=0, keepdims=True)
        dests.append(valid * (e_lane[k] * float(seq) + base + slot))
        gates.append(to_lanes(p_sub[k] / total))
    row = lax.broadcasted_iota(jnp.int32, (table_rows, lanes), 0)
    mine = lax.div(me, per_row)
    n_rows = table_rows // 4
    table = jnp.zeros((table_rows, lanes), jnp.float32)
    for n, vec in enumerate(dests + gates):
        table = jnp.where(row == n * n_rows + mine, vec, table)
    return table


def build_kernel(h_ref, table_ref, out_ref, hid_ref, zeros, slots, hid_buf, sems, hid_sem):
    me = lax.axis_index('sp')
    experts_dev, seq, width = out_ref.shape
    n_chips, n_cols, tok_chip, cols = h_ref.shape
    tok_dev = hid_ref.shape[0]
    n_groups = sems.shape[0]
    per_expert = n_groups // experts_dev
    n_rows = table_ref.shape[0] // 4
    lanes = table_ref.shape[1]

    per_chip = tok_chip // tok_dev
    chip = lax.div(me, per_chip)
    first = pl.multiple_of(lax.rem(me, per_chip) * tok_dev, tok_dev)
    for n in range(n_cols):
        hid_buf[:, n * cols:(n + 1) * cols] = h_ref[chip, n, pl.ds(first, tok_dev), :]
    hid_copy = pltpu.make_async_copy(hid_buf, hid_ref, hid_sem)
    hid_copy.start()
    zeros[...] = jnp.zeros_like(zeros)

    table = table_ref[...]
    base = me * experts_dev * seq
    group_first = (base + GROUP_ROWS * lax.broadcasted_iota(jnp.int32, (n_groups, lanes), 0)).astype(jnp.float32)
    hits = jnp.zeros((n_groups, lanes), jnp.float32)
    for r in range(2 * n_rows):
        dest = table[r:r + 1, :]
        hits = jnp.where((dest >= group_first) & (dest < group_first + float(GROUP_ROWS)), 1.0, hits)
    used = jnp.max(hits, axis=1, keepdims=True)
    power = lax.shift_left(jnp.ones((n_groups, 1), jnp.int32), lax.broadcasted_iota(jnp.int32, (n_groups, 1), 0))
    used_bits = jnp.sum(used * power.astype(jnp.float32)).astype(jnp.int32)

    def is_used(n):
        return lax.rem(lax.shift_right_logical(used_bits, n), 2) == 1

    def put(src, n):
        expert, part = lax.div(n, per_expert), lax.rem(n, per_expert)
        at = pl.ds(pl.multiple_of(part * GROUP_ROWS, GROUP_ROWS), GROUP_ROWS)
        return pltpu.make_async_copy(src, out_ref.at[expert, at], sems.at[n])

    def put_zeros(n, carry):
        @pl.when(jnp.logical_not(is_used(n)))
        def _():
            put(zeros, n).start()
        return carry

    lax.fori_loop(0, n_groups, put_zeros, 0)

    spread = lambda n: jnp.concatenate([table[n * n_rows + r:n * n_rows + r + 1, :] for r in range(n_rows)], axis=1)
    dest = [spread(0), spread(1)]
    gate = [spread(2), spread(3)]

    def put_rows(n, carry):
        @pl.when(is_used(n))
        def _():
            row = (lax.broadcasted_iota(jnp.int32, (GROUP_ROWS, seq), 0) + (base + n * GROUP_ROWS)).astype(jnp.float32)
            hit = [dest[0] == row, dest[1] == row]
            gate_row = jnp.sum(jnp.where(hit[0], gate[0], 0.0) + jnp.where(hit[1], gate[1], 0.0), axis=1, keepdims=True)
            pick = jnp.where(hit[0] | hit[1], 1.0, 0.0).astype(jnp.bfloat16)
            for c in range(n_cols):
                rows = h_ref[:, c].reshape(seq, cols)
                got = jnp.dot(pick, rows, preferred_element_type=jnp.float32)
                slots[n, :, c * cols:(c + 1) * cols] = (got * gate_row).astype(jnp.bfloat16)
            put(slots.at[n], n).start()
        return carry

    lax.fori_loop(0, n_groups, put_rows, 0)

    def wait_group(n, carry):
        put(zeros, n).wait()
        return carry

    lax.fori_loop(0, n_groups, wait_group, 0)
    hid_copy.wait()


def build_buffers(h_all, table, tok_dev, experts_dev):
    n_chips, n_cols, tok_chip, cols = h_all.shape
    seq, width = n_chips * tok_chip, n_cols * cols
    n_groups = experts_dev * seq // GROUP_ROWS
    bf16 = jnp.bfloat16
    in_vmem = pl.BlockSpec(memory_space=pltpu.VMEM)
    anywhere = pl.BlockSpec(memory_space=pl.ANY)
    dma = pltpu.SemaphoreType.DMA
    return pl.pallas_call(
        build_kernel,
        name='build_buffers',
        in_specs=[in_vmem, in_vmem],
        out_specs=[anywhere, anywhere],
        out_shape=[jax.ShapeDtypeStruct((experts_dev, seq, width), bf16), jax.ShapeDtypeStruct((tok_dev, width), bf16)],
        scratch_shapes=[
            pltpu.VMEM((GROUP_ROWS, width), bf16), pltpu.VMEM((n_groups, GROUP_ROWS, width), bf16), pltpu.VMEM((tok_dev, width), bf16),
            dma((n_groups,)), dma,
        ],
        compiler_params=pltpu.CompilerParams(vmem_limit_bytes=40 * 1024 * 1024),
        cost_estimate=pl.CostEstimate(flops=2 * experts_dev * seq * seq * width, bytes_accessed=2 * experts_dev * seq * width, transcendentals=0),
    )(h_all, table)


def block_kernel(x_hbm, wq, wk, wv, wo, ids_hbm, probs_hbm, h_all, table_out, wbuf, x_buf, kv, q_buf, o_buf, tab_pair, tabs, ids, probs,
                 w_sem, in_sem, pair_send, pair_recv, kv_send, kv_recv, tab_send, tab_recv, o_send, o_recv, h_send, h_recv, d_send, d_recv):
    tok_dev, width = x_hbm.shape
    chips = kv.shape[0]
    tok_chip = x_buf.shape[0]
    seq = chips * tok_chip
    heads_core = q_buf.shape[0]
    kv_core = kv.shape[3] // HEAD_DIM
    per_kv = heads_core // kv_core
    q_core = heads_core * HEAD_DIM
    out_core = width // 2
    fwd, bwd = chips // 2, chips // 2 - 1
    me = lax.axis_index('sp')
    chip, core = lax.div(me, 2), lax.rem(me, 2)
    other = 1 - core
    partner = {'sp': 2 * chip + other}

    def far(step):
        return {'sp': 2 * lax.rem(chip + chips + step, chips) + core}

    def remote(src, dst, send, recv, device):
        return pltpu.make_async_remote_copy(src_ref=src, dst_ref=dst, send_sem=send, recv_sem=recv, device_id=device, device_id_type=MESH)

    barrier = pltpu.get_barrier_semaphore()
    near = [partner, far(1), far(-1), far(2), far(-2)]
    for device in near:
        pl.semaphore_signal(barrier, inc=1, device_id=device, device_id_type=MESH)

    n_slots = wbuf.shape[0]
    kv_units = 2 * (kv.shape[3] // COLS) * (width // ROWS)
    half_units = q_core // ROWS
    chunk_units = 2 * half_units
    in_units = width // ROWS
    q_chunks = q_core // COLS
    o_chunks = out_core // COLS
    kv_chunks = kv.shape[3] // COLS

    def load(src, row, col, slot):
        return pltpu.make_async_copy(src.at[pl.ds(row, ROWS), pl.ds(pl.multiple_of(col, COLS), COLS)], wbuf.at[slot], w_sem.at[slot])

    def wait_unit(slot):
        load(wk, 0, 0, slot).wait()

    def start_q(n):
        for r in range(in_units):
            load(wq, r * ROWS, core * q_core + n * COLS, lax.rem(kv_units + in_units * n + r, n_slots)).start()

    first_o = kv_units + in_units * q_chunks - n_slots

    def start_o(k):
        j, r = lax.div(k, chunk_units), lax.rem(k, chunk_units)
        half = jnp.where(r < half_units, core, other)
        row = pl.multiple_of(half * q_core + lax.rem(r, half_units) * ROWS, ROWS)
        load(wo, row, core * out_core + j * COLS, first_o + k).start()

    own = pl.ds(pl.multiple_of(core * tok_dev, tok_dev), tok_dev)
    theirs = pl.ds(pl.multiple_of(other * tok_dev, tok_dev), tok_dev)
    x_in = pltpu.make_async_copy(x_hbm, x_buf.at[own], in_sem.at[0])
    x_in.start()
    slot = 0
    for src in (wk, wv):
        for n in range(kv_chunks):
            for r in range(in_units):
                load(src, r * ROWS, core * kv.shape[3] + n * COLS, slot).start()
                slot += 1
    ids_in = pltpu.make_async_copy(ids_hbm, ids, in_sem.at[1])
    probs_in = pltpu.make_async_copy(probs_hbm, probs, in_sem.at[2])
    ids_in.start()
    probs_in.start()
    x_in.wait()
    pl.semaphore_wait(barrier, len(near))

    x_pair = remote(x_buf.at[own], x_buf.at[own], pair_send.at[0], pair_recv.at[0], partner)
    x_pair.start()
    q_first = (n_slots - kv_units) // in_units
    lax.fori_loop(0, q_first, lambda n, c: (start_q(n), c)[1], 0)
    remote(x_buf.at[theirs], x_buf.at[theirs], pair_send.at[0], pair_recv.at[0], partner).wait_recv()

    def project(pair_slot):
        for r in range(in_units):
            wait_unit(pair_slot + r)
        w = wbuf[pl.ds(pair_slot, in_units)].reshape(width, COLS)
        return jnp.dot(x_buf[...], w, preferred_element_type=jnp.float32).astype(jnp.bfloat16)

    def kv_piece(block, which):
        return kv.at[block, which]

    def tab_piece(block, which):
        return tabs.at[block]

    def ring(piece, sends, recvs, which, s, back, arriving=0):
        s_at = s + arriving
        block = lax.rem(chip + s_at, chips) if back else lax.rem(chip + chips - s_at, chips)
        part = piece(block, which)
        return remote(part, part, sends.at[which, 4 * back + s], recvs.at[which, 4 * back + s], far(-1) if back else far(1))

    def ring_start(*args):
        ring(*args, 0, 0).start()
        ring(*args, 0, 1).start()

    def ring_hop(*args):
        *args, s = args
        ring(*args, s, 0, 1).wait_recv()
        if s + 1 < fwd:
            ring(*args, s + 1, 0).start()
        if s < bwd:
            ring(*args, s, 1, 1).wait_recv()
            if s + 1 < bwd:
                ring(*args, s + 1, 1).start()

    kv_ring = (kv_piece, kv_send, kv_recv)
    tab_ring = (tab_piece, tab_send, tab_recv)

    slot = 0
    for which in range(2):
        for n in range(kv_chunks):
            kv[chip, which, :, n * COLS:(n + 1) * COLS] = project(slot)
            slot += in_units
        ring_start(*kv_ring, which)

    for n in range(q_first, q_chunks):
        start_q(n)
    early = kv_units - first_o
    for k in range(early):
        start_o(k)

    ids_in.wait()
    probs_in.wait()
    tab_pair[0] = route_table(me, ids[...], probs[...], seq, tab_pair.shape[1])
    t_pair = remote(tab_pair.at[0], tab_pair.at[1], pair_send.at[1], pair_recv.at[1], partner)
    t_pair.start()

    heads_chunk = COLS // HEAD_DIM

    def q_step(n, carry):
        res = project(lax.rem(kv_units + in_units * n, n_slots))
        for i in range(heads_chunk):
            q_buf[heads_chunk * n + i] = res[:, i * HEAD_DIM:(i + 1) * HEAD_DIM]

        @pl.when(n < q_first)
        def _():
            for r in range(in_units):
                start_o(early + in_units * n + r)
        return carry

    at = 0
    for s in range(fwd):
        for which in range(2):
            upto = q_chunks * (2 * s + which + 1) // (2 * fwd)
            upto = min(q_chunks, upto + (1 if s == 0 else 0))
            lax.fori_loop(at, upto, q_step, 0)
            at = upto
            ring_hop(*kv_ring, which, s)
        if s == 0:
            t_pair.wait_recv()
            tabs[chip] = tab_pair[0] + tab_pair[1]
            ring_start(*tab_ring, 0)
        else:
            ring_hop(*tab_ring, 0, s - 1)

    rows = per_kv * tok_chip
    q_pos = tok_chip * chip + lax.rem(lax.broadcasted_iota(jnp.int32, (rows, seq), 0), tok_chip)
    seen = lax.broadcasted_iota(jnp.int32, (rows, seq), 1) <= q_pos
    o_copies = []
    for g in range(kv_core):
        lanes = slice(g * HEAD_DIM, (g + 1) * HEAD_DIM)
        qg = q_buf[g * per_kv:(g + 1) * per_kv].reshape(rows, HEAD_DIM)
        kg = kv[:, 0, :, lanes].reshape(seq, HEAD_DIM)
        vg = kv[:, 1, :, lanes].reshape(seq, HEAD_DIM)
        s = lax.dot_general(qg, kg, (((1,), (1,)), ((), ())), preferred_element_type=jnp.float32) * SCORE_SCALE
        s = jnp.where(seen, s, -1e30)
        p = jnp.exp(s - jnp.max(s, axis=1, keepdims=True))
        p = (p / jnp.sum(p, axis=1, keepdims=True)).astype(jnp.bfloat16)
        o = jnp.dot(p, vg, preferred_element_type=jnp.float32).astype(jnp.bfloat16)
        for h in range(per_kv):
            col = (g * per_kv + h) * HEAD_DIM
            o_buf[0, :, col:col + HEAD_DIM] = o[h * tok_chip:(h + 1) * tok_chip]
        span = pl.ds(g * per_kv * HEAD_DIM, per_kv * HEAD_DIM)
        copy = remote(o_buf.at[0, :, span], o_buf.at[1, :, span], o_send.at[g], o_recv.at[g], partner)
        copy.start()
        o_copies.append(copy)
    ring_hop(*tab_ring, 0, fwd - 1)

    def h_copy(j, source, reach, step, back):
        block = lax.rem(chip + source, chips) if back else lax.rem(chip + chips - source, chips)
        piece = h_all.at[block, core * o_chunks + j]
        if reach == fwd:
            piece = piece.at[pl.ds(back * tok_dev, tok_dev)]
        n = 4 * back + reach - 1
        return remote(piece, piece, h_send.at[j, n], h_recv.at[j, n], far(-step) if back else far(step))

    def h_sends(j):
        if j < CHAIN:
            return [(reach - 1, reach, 1) for reach in range(1, fwd + 1)]
        return [(0, 1, 1), (0, 2, 2)] + [(2, reach, reach - 2) for reach in range(3, fwd + 1)]

    def h_start(j, source):
        for back in range(2):
            for src, reach, step in h_sends(j):
                if src == source:
                    h_copy(j, src, reach, step, back).start()

    def h_arrive(j, reach):
        for back in range(2):
            h_copy(j, reach, reach, 1, back).wait_recv()
            for src, onward, step in h_sends(j):
                if src == reach:
                    h_copy(j, src, onward, step, back).start()
        if reach == fwd:
            h_pair(j, core).start()

    def h_pair(j, half):
        cols = h_all.at[:, half * o_chunks + j]
        return remote(cols, cols, d_send.at[j], d_recv.at[j], partner)

    def due(t):
        steps = []
        for j in range(o_chunks):
            for reach in range(1, fwd + 1):
                when = j + LAG * reach if j < CHAIN else j + LAG * (2 if reach > 2 else 1)
                if when == t:
                    steps.append((j, reach))
        return steps

    for j in range(o_chunks):
        at = first_o + chunk_units * j
        for r in range(half_units):
            wait_unit(at + r)
        acc = jnp.dot(o_buf[0], wbuf[pl.ds(at, half_units)].reshape(q_core, COLS), preferred_element_type=jnp.float32)
        if j == 0:
            for copy in o_copies:
                copy.wait_recv()
        for r in range(half_units):
            wait_unit(at + half_units + r)
        acc += jnp.dot(o_buf[1], wbuf[pl.ds(at + half_units, half_units)].reshape(q_core, COLS), preferred_element_type=jnp.float32)
        x_cols = x_buf[:, pl.ds(pl.multiple_of(core * out_core + j * COLS, COLS), COLS)]
        h_all[chip, core * o_chunks + j] = (x_cols.astype(jnp.float32) + acc).astype(jnp.bfloat16)
        h_start(j, 0)
        for step in due(j):
            h_arrive(*step)

    table_out[...] = jnp.sum(tabs[...], axis=0)
    for t in range(o_chunks, o_chunks + LAG * fwd):
        for step in due(t):
            h_arrive(*step)
    for j in range(o_chunks):
        h_pair(j, other).wait_recv()

    x_pair.wait_send()
    t_pair.wait_send()
    for args in ((*kv_ring, 0), (*kv_ring, 1), (*tab_ring, 0)):
        for back, hops in ((0, fwd), (1, bwd)):
            for s in range(hops):
                ring(*args, s, back).wait_send()
    for copy in o_copies:
        copy.wait_send()
    for j in range(o_chunks):
        for back in range(2):
            for src, reach, step in h_sends(j):
                h_copy(j, src, reach, step, back).wait_send()
        h_pair(j, core).wait_send()


def attend(x_loc, w_q, w_k, w_v, w_o, ids, probs, group):
    tok_dev, width = x_loc.shape
    chips = group // 2
    tok_chip = 2 * tok_dev
    heads_core = w_q.shape[1] // HEAD_DIM // 2
    kv_width = w_k.shape[1] // 2
    q_core = heads_core * HEAD_DIM
    lanes = probs.shape[1]
    table_rows = 4 * chips * tok_chip // lanes
    o_chunks = width // 2 // COLS
    kv_core = kv_width // HEAD_DIM
    kv_units = 2 * kv_width // COLS * (width // ROWS)
    units = kv_units + (q_core // COLS) * (width // ROWS) + o_chunks * 2 * q_core // ROWS
    n_slots = units // 2
    bf16, f32 = jnp.bfloat16, jnp.float32
    dma = pltpu.SemaphoreType.DMA
    anywhere = pl.BlockSpec(memory_space=pl.ANY)
    in_vmem = pl.BlockSpec(memory_space=pltpu.VMEM)
    return pl.pallas_call(
        block_kernel,
        name='attend',
        in_specs=[anywhere] * 7,
        out_specs=[in_vmem, in_vmem],
        out_shape=[pltpu.VMEM((chips, width // COLS, tok_chip, COLS), bf16), pltpu.VMEM((table_rows, lanes), f32)],
        scratch_shapes=[
            pltpu.VMEM((n_slots, ROWS, COLS), bf16),
            pltpu.VMEM((tok_chip, width), bf16),
            pltpu.VMEM((chips, 2, tok_chip, kv_width), bf16),
            pltpu.VMEM((heads_core, tok_chip, HEAD_DIM), bf16),
            pltpu.VMEM((2, tok_chip, q_core), bf16),
            pltpu.VMEM((2, table_rows, lanes), f32),
            pltpu.VMEM((chips, table_rows, lanes), f32),
            pltpu.VMEM(ids.shape, ids.dtype),
            pltpu.VMEM(probs.shape, probs.dtype),
            dma((n_slots,)), dma((3,)), dma((2,)), dma((2,)), dma((2, 8)), dma((2, 8)), dma((1, 8)), dma((1, 8)), dma((kv_core,)), dma((kv_core,)),
            dma((o_chunks, 8)), dma((o_chunks, 8)), dma((o_chunks,)), dma((o_chunks,)),
        ],
        compiler_params=pltpu.CompilerParams(collective_id=0, has_side_effects=True, vmem_limit_bytes=60_000_000),
    )(x_loc, w_q, w_k, w_v, w_o, ids, probs)


def solution(mesh):
    group = mesh.shape['sp']
    row_spec = P(('dp', 'sp'), None)
    buf_spec = P(('dp', 'sp'), None, None)

    def device_step(x_loc, w_q, w_k, w_v, w_o, ids_loc, probs_loc):
        h_all, table = attend(x_loc, w_q, w_k, w_v, w_o, ids_loc.T, probs_loc, group)
        buf, hid = build_buffers(h_all, table, x_loc.shape[0], probs_loc.shape[1] // group)
        return hid, buf

    return jax.shard_map(device_step, mesh=mesh, in_specs=(row_spec, P(), P(), P(), P(), row_spec, row_spec), out_specs=(row_spec, buf_spec), check_vma=False)
```

time: 77.3 us -> 66.8 us (0.86)
  Pallas kernels: 73.2 us -> 65.9 us
  local copies, waits for them, and re-layouts: 3.62 us -> 0 us
    pallas_call x2, Pallas kernels: 73.2 us -> 65.9 us  [the longest x1 59.7 us: attend(): pl.pallas_call(block_kernel, name='attend', in_specs=[anywhere] * 7, out_...]
    unnamed x5 -> x0, local copies, waits for them, and re-layouts: 3.62 us -> none
where the time goes in v3:
time: 66.8 us; the launch traced here: 66.7 us
  Pallas kernels  65.9 us (99%)
  between operations  0.8 us (1%)
    pallas_call x1, Pallas kernels, attend(): pl.pallas_call(block_kernel, name='attend', in_specs=[anywhere] * 7, out_...  59.7 us
    pallas_call x1, Pallas kernels, build_buffers(): pl.pallas_call(build_kernel, name='build_buffers', in_specs=[in_vmem, in_...  6.22 us

profile of v3, /device:TPU:21, one launch (start us, length us, event | category | flops | bytes accessed | tf_op | source)
XLA Modules:
  0.0 66.7 jit_solution(12322210246028033420)
XLA Ops:
  0.6 59.7 %attend.1 = (bf16[8,16,32,256]{3,2,1,0:T(8,128)(2,1)S(1)}, f32[8,128]{1,0:T(8,128)S(1)}) custom-call(bf16[16,4096]{1,0:T(8,128)(2,1)} %x_hbm.1, bf16[4096,12288]{1,0:T(8,128)(2,1)} %wq.1, bf16[4096,1024]{1,0:T(8,128)(2,1)} %wk.1, bf16[4096,1024]{1,0:T(8,128)(2,1)} %wv.1, bf16[12288,4096]{1,0:T(8,128)(2,1)} %wo.1, s32[2,16]{1,0:T(2,128)} %bitcast.1, ...), custom_call_target="tpu_custom_call" | custom-call | tf_op jit(solution)/shard_map/attend/pallas_call | solution.py:430
  60.3 6.2 %build_buffers.1 = (bf16[8,256,4096]{2,1,0:T(8,128)(2,1)}, bf16[16,4096]{1,0:T(8,128)(2,1)}) custom-call(bf16[8,16,32,256]{3,2,1,0:T(8,128)(2,1)S(1)} %get-tuple-element.6.h_ref, f32[8,128]{1,0:T(8,128)S(1)} %get-tuple-element.7.table_ref), custom_call_target="tpu_custom_call" | custom-call | flops 4294967296 | bytes 16777216 | tf_op jit(solution)/shard_map/build_buffers/pallas_call | solution.py:134

commit v4 on v3

--- a/solution.py
+++ b/solution.py
@@ -12,7 +12,8 @@
 COLS = 256
 ROWS = 2048
 LAG = 2
-CHAIN = 4
+Q_STOPS = (8, 11)
+CHAIN = 3
 GROUP_ROWS = 128
 MESH = pl.DeviceIdType.MESH
 
@@ -230,8 +231,42 @@
         w = wbuf[pl.ds(pair_slot, in_units)].reshape(width, COLS)
         return jnp.dot(x_buf[...], w, preferred_element_type=jnp.float32).astype(jnp.bfloat16)
 
+    def two_step(piece, sends, recvs, n, source, reach, step, back):
+        block = lax.rem(chip + source, chips) if back else lax.rem(chip + chips - source, chips)
+        part = piece(block, n)
+        if reach == fwd:
+            part = part.at[pl.ds(back * tok_dev, tok_dev)]
+        at = 4 * back + reach - 1
+        return remote(part, part, sends.at[n, at], recvs.at[n, at], far(-step) if back else far(step))
+
+    def two_step_start(*args):
+        for reach in (1, 2):
+            for back in range(2):
+                two_step(*args, 0, reach, reach, back).start()
+
+    def two_step_onward(*args):
+        for back in range(2):
+            two_step(*args, 2, 2, 2, back).wait_recv()
+            for reach in range(3, fwd + 1):
+                two_step(*args, 2, reach, reach - 2, back).start()
+        for back in range(2):
+            two_step(*args, 1, 1, 1, back).wait_recv()
+
+    def two_step_last(*args):
+        for reach in range(3, fwd + 1):
+            for back in range(2):
+                two_step(*args, reach, reach, 1, back).wait_recv()
+
+    def two_step_sent(*args):
+        for back in range(2):
+            for reach in range(1, fwd + 1):
+                two_step(*args, 0 if reach < 3 else 2, reach, 1, back).wait_send()
+
     def kv_piece(block, which):
         return kv.at[block, which]
+
+    def h_piece(block, j):
+        return h_all.at[block, core * o_chunks + j]
 
     def tab_piece(block, which):
         return tabs.at[block]
@@ -264,7 +299,7 @@
         for n in range(kv_chunks):
             kv[chip, which, :, n * COLS:(n + 1) * COLS] = project(slot)
             slot += in_units
-        ring_start(*kv_ring, which)
+        two_step_start(*kv_ring, which)
 
     for n in range(q_first, q_chunks):
         start_q(n)
@@ -291,20 +326,18 @@
                 start_o(early + in_units * n + r)
         return carry
 
-    at = 0
-    for s in range(fwd):
-        for which in range(2):
-            upto = q_chunks * (2 * s + which + 1) // (2 * fwd)
-            upto = min(q_chunks, upto + (1 if s == 0 else 0))
-            lax.fori_loop(at, upto, q_step, 0)
-            at = upto
-            ring_hop(*kv_ring, which, s)
-        if s == 0:
-            t_pair.wait_recv()
-            tabs[chip] = tab_pair[0] + tab_pair[1]
-            ring_start(*tab_ring, 0)
-        else:
-            ring_hop(*tab_ring, 0, s - 1)
+    lax.fori_loop(0, Q_STOPS[0], q_step, 0)
+    t_pair.wait_recv()
+    tabs[chip] = tab_pair[0] + tab_pair[1]
+    ring_start(*tab_ring, 0)
+    two_step_onward(*kv_ring, 0)
+    lax.fori_loop(Q_STOPS[0], Q_STOPS[1], q_step, 0)
+    two_step_onward(*kv_ring, 1)
+    ring_hop(*tab_ring, 0, 0)
+    lax.fori_loop(Q_STOPS[1], q_chunks, q_step, 0)
+    ring_hop(*tab_ring, 0, 1)
+    for which in range(2):
+        two_step_last(*kv_ring, which)
 
     rows = per_kv * tok_chip
     q_pos = tok_chip * chip + lax.rem(lax.broadcasted_iota(jnp.int32, (rows, seq), 0), tok_chip)
@@ -327,55 +360,34 @@
         copy = remote(o_buf.at[0, :, span], o_buf.at[1, :, span], o_send.at[g], o_recv.at[g], partner)
         copy.start()
         o_copies.append(copy)
-    ring_hop(*tab_ring, 0, fwd - 1)
-
-    def h_copy(j, source, reach, step, back):
-        block = lax.rem(chip + source, chips) if back else lax.rem(chip + chips - source, chips)
-        piece = h_all.at[block, core * o_chunks + j]
-        if reach == fwd:
-            piece = piece.at[pl.ds(back * tok_dev, tok_dev)]
-        n = 4 * back + reach - 1
-        return remote(piece, piece, h_send.at[j, n], h_recv.at[j, n], far(-step) if back else far(step))
-
-    def h_sends(j):
-        if j < CHAIN:
-            return [(reach - 1, reach, 1) for reach in range(1, fwd + 1)]
-        return [(0, 1, 1), (0, 2, 2)] + [(2, reach, reach - 2) for reach in range(3, fwd + 1)]
-
-    def h_start(j, source):
+    ring_hop(*tab_ring, 0, 2)
+
+    h_ring = (h_piece, h_send, h_recv)
+
+    def chain_hop(j, reach):
         for back in range(2):
-            for src, reach, step in h_sends(j):
-                if src == source:
-                    h_copy(j, src, reach, step, back).start()
-
-    def h_arrive(j, reach):
-        for back in range(2):
-            h_copy(j, reach, reach, 1, back).wait_recv()
-            for src, onward, step in h_sends(j):
-                if src == reach:
-                    h_copy(j, src, onward, step, back).start()
+            two_step(*h_ring, j, reach, reach, 1, back).wait_recv()
+            if reach < fwd:
+                two_step(*h_ring, j, reach, reach + 1, 1, back).start()
         if reach == fwd:
             h_pair(j, core).start()
+
+    def last_step(j):
+        two_step_last(*h_ring, j)
+        h_pair(j, core).start()
 
     def h_pair(j, half):
         cols = h_all.at[:, half * o_chunks + j]
         return remote(cols, cols, d_send.at[j], d_recv.at[j], partner)
 
-    def due(t):
-        steps = []
-        for j in range(o_chunks):
-            for reach in range(1, fwd + 1):
-                when = j + LAG * reach if j < CHAIN else j + LAG * (2 if reach > 2 else 1)
-                if when == t:
-                    steps.append((j, reach))
-        return steps
-
-    for j in range(o_chunks):
+    def o_step(j, carry):
         at = first_o + chunk_units * j
         for r in range(half_units):
             wait_unit(at + r)
         acc = jnp.dot(o_buf[0], wbuf[pl.ds(at, half_units)].reshape(q_core, COLS), preferred_element_type=jnp.float32)
-        if j == 0:
+
+        @pl.when(j == 0)
+        def _():
             for copy in o_copies:
                 copy.wait_recv()
         for r in range(half_units):
@@ -383,30 +395,61 @@
         acc += jnp.dot(o_buf[1], wbuf[pl.ds(at + half_units, half_units)].reshape(q_core, COLS), preferred_element_type=jnp.float32)
         x_cols = x_buf[:, pl.ds(pl.multiple_of(core * out_core + j * COLS, COLS), COLS)]
         h_all[chip, core * o_chunks + j] = (x_cols.astype(jnp.float32) + acc).astype(jnp.bfloat16)
-        h_start(j, 0)
-        for step in due(j):
-            h_arrive(*step)
-
+        for back in range(2):
+            two_step(*h_ring, j, 0, 1, 1, back).start()
+
+        @pl.when(j >= CHAIN)
+        def _():
+            for back in range(2):
+                two_step(*h_ring, j, 0, 2, 2, back).start()
+
+        for reach in range(1, fwd):
+            late = j - LAG * reach
+
+            @pl.when((late >= 0) & (late < CHAIN))
+            def _(late=late, reach=reach):
+                chain_hop(late, reach)
+
+        @pl.when(j >= CHAIN + LAG)
+        def _():
+            two_step_onward(*h_ring, j - LAG)
+
+        @pl.when(j >= CHAIN + 2 * LAG)
+        def _():
+            last_step(j - 2 * LAG)
+        return carry
+
+    lax.fori_loop(0, o_chunks, o_step, 0)
+    for reach in range(1, fwd):
+        for j in range(max(0, o_chunks - LAG * reach), CHAIN):
+            chain_hop(j, reach)
+    for j in range(o_chunks - LAG, o_chunks):
+        two_step_onward(*h_ring, j)
+    ring_hop(*tab_ring, 0, fwd - 1)
     table_out[...] = jnp.sum(tabs[...], axis=0)
-    for t in range(o_chunks, o_chunks + LAG * fwd):
-        for step in due(t):
-            h_arrive(*step)
+    for j in range(CHAIN):
+        chain_hop(j, fwd)
+    for j in range(max(CHAIN, o_chunks - 2 * LAG), o_chunks):
+        last_step(j)
     for j in range(o_chunks):
         h_pair(j, other).wait_recv()
 
     x_pair.wait_send()
     t_pair.wait_send()
-    for args in ((*kv_ring, 0), (*kv_ring, 1), (*tab_ring, 0)):
-        for back, hops in ((0, fwd), (1, bwd)):
-            for s in range(hops):
-                ring(*args, s, back).wait_send()
+    for back, hops in ((0, fwd), (1, bwd)):
+        for n in range(hops):
+            ring(*tab_ring, 0, n, back).wait_send()
+    for which in range(2):
+        two_step_sent(*kv_ring, which)
     for copy in o_copies:
         copy.wait_send()
-    for j in range(o_chunks):
-        for back in range(2):
-            for src, reach, step in h_sends(j):
-                h_copy(j, src, reach, step, back).wait_send()
+
+    def sent(j, carry):
+        two_step_sent(*h_ring, j)
         h_pair(j, core).wait_send()
+        return carry
+
+    lax.fori_loop(0, o_chunks, sent, 0)
 
 
 def attend(x_loc, w_q, w_k, w_v, w_o, ids, probs, group):
@@ -446,7 +489,7 @@
             dma((n_slots,)), dma((3,)), dma((2,)), dma((2,)), dma((2, 8)), dma((2, 8)), dma((1, 8)), dma((1, 8)), dma((kv_core,)), dma((kv_core,)),
             dma((o_chunks, 8)), dma((o_chunks, 8)), dma((o_chunks,)), dma((o_chunks,)),
         ],
-        compiler_params=pltpu.CompilerParams(collective_id=0, has_side_effects=True, vmem_limit_bytes=60_000_000),
+        compiler_params=pltpu.CompilerParams(collective_id=0, has_side_effects=True, vmem_limit_bytes=63_000_000),
     )(x_loc, w_q, w_k, w_v, w_o, ids, probs)
 
 

time: 66.8 us -> 61.2 us (0.916)
  Pallas kernels: 65.9 us -> 60.4 us
    pallas_call x1, Pallas kernels: 59.7 us -> 54.2 us  [attend(): pl.pallas_call(block_kernel, name='attend', in_specs=[anywhere] * 7, out_...]
where the time goes in v4:
time: 61.2 us; the launch traced here: 61.1 us
  Pallas kernels  60.4 us (99%)
  between operations  0.64 us (1%)
    pallas_call x1, Pallas kernels, attend(): pl.pallas_call(block_kernel, name='attend', in_specs=[anywhere] * 7, out_...  54.2 us
    pallas_call x1, Pallas kernels, build_buffers(): pl.pallas_call(build_kernel, name='build_buffers', in_specs=[in_vmem, in_...  6.22 us

profile of v4, /device:TPU:21, one launch (start us, length us, event | category | flops | bytes accessed | tf_op | source)
XLA Modules:
  0.0 61.1 jit_solution(6624577108630987768)
XLA Ops:
  0.6 54.2 %attend.1 = (bf16[8,16,32,256]{3,2,1,0:T(8,128)(2,1)S(1)}, f32[8,128]{1,0:T(8,128)S(1)}) custom-call(bf16[16,4096]{1,0:T(8,128)(2,1)} %x_hbm.1, bf16[4096,12288]{1,0:T(8,128)(2,1)} %wq.1, bf16[4096,1024]{1,0:T(8,128)(2,1)} %wk.1, bf16[4096,1024]{1,0:T(8,128)(2,1)} %wv.1, bf16[12288,4096]{1,0:T(8,128)(2,1)} %wo.1, s32[2,16]{1,0:T(2,128)} %bitcast.1, ...), custom_call_target="tpu_custom_call" | custom-call | tf_op jit(solution)/shard_map/attend/pallas_call | solution.py:473
  54.9 6.2 %build_buffers.1 = (bf16[8,256,4096]{2,1,0:T(8,128)(2,1)}, bf16[16,4096]{1,0:T(8,128)(2,1)}) custom-call(bf16[8,16,32,256]{3,2,1,0:T(8,128)(2,1)S(1)} %get-tuple-element.6.h_ref, f32[8,128]{1,0:T(8,128)S(1)} %get-tuple-element.7.table_ref), custom_call_target="tpu_custom_call" | custom-call | flops 4294967296 | bytes 16777216 | tf_op jit(solution)/shard_map/build_buffers/pallas_call | solution.py:135

commit v5 on v4

--- a/solution.py
+++ b/solution.py
@@ -12,8 +12,8 @@
 COLS = 256
 ROWS = 2048
 LAG = 2
-Q_STOPS = (8, 11)
-CHAIN = 3
+Q_STOPS = (5, 7)
+CHAIN = 2
 GROUP_ROWS = 128
 MESH = pl.DeviceIdType.MESH
 
@@ -60,13 +60,6 @@
     n_rows = table_ref.shape[0] // 4
     lanes = table_ref.shape[1]
 
-    per_chip = tok_chip // tok_dev
-    chip = lax.div(me, per_chip)
-    first = pl.multiple_of(lax.rem(me, per_chip) * tok_dev, tok_dev)
-    for n in range(n_cols):
-        hid_buf[:, n * cols:(n + 1) * cols] = h_ref[chip, n, pl.ds(first, tok_dev), :]
-    hid_copy = pltpu.make_async_copy(hid_buf, hid_ref, hid_sem)
-    hid_copy.start()
     zeros[...] = jnp.zeros_like(zeros)
 
     table = table_ref[...]
@@ -95,6 +88,14 @@
         return carry
 
     lax.fori_loop(0, n_groups, put_zeros, 0)
+
+    per_chip = tok_chip // tok_dev
+    chip = lax.div(me, per_chip)
+    first = pl.multiple_of(lax.rem(me, per_chip) * tok_dev, tok_dev)
+    for n in range(n_cols):
+        hid_buf[:, n * cols:(n + 1) * cols] = h_ref[chip, n, pl.ds(first, tok_dev), :]
+    hid_copy = pltpu.make_async_copy(hid_buf, hid_ref, hid_sem)
+    hid_copy.start()
 
     spread = lambda n: jnp.concatenate([table[n * n_rows + r:n * n_rows + r + 1, :] for r in range(n_rows)], axis=1)
     dest = [spread(0), spread(1)]
@@ -206,6 +207,7 @@
     theirs = pl.ds(pl.multiple_of(other * tok_dev, tok_dev), tok_dev)
     x_in = pltpu.make_async_copy(x_hbm, x_buf.at[own], in_sem.at[0])
     x_in.start()
+    x_in.wait()
     slot = 0
     for src in (wk, wv):
         for n in range(kv_chunks):
@@ -216,7 +218,6 @@
     probs_in = pltpu.make_async_copy(probs_hbm, probs, in_sem.at[2])
     ids_in.start()
     probs_in.start()
-    x_in.wait()
     pl.semaphore_wait(barrier, len(near))
 
     x_pair = remote(x_buf.at[own], x_buf.at[own], pair_send.at[0], pair_recv.at[0], partner)
@@ -225,9 +226,11 @@
     lax.fori_loop(0, q_first, lambda n, c: (start_q(n), c)[1], 0)
     remote(x_buf.at[theirs], x_buf.at[theirs], pair_send.at[0], pair_recv.at[0], partner).wait_recv()
 
+    def wait_units(first, count):
+        for r in range(count):
+            wait_unit(first + r)
+
     def project(pair_slot):
-        for r in range(in_units):
-            wait_unit(pair_slot + r)
         w = wbuf[pl.ds(pair_slot, in_units)].reshape(width, COLS)
         return jnp.dot(x_buf[...], w, preferred_element_type=jnp.float32).astype(jnp.bfloat16)
 
@@ -297,6 +300,7 @@
     slot = 0
     for which in range(2):
         for n in range(kv_chunks):
+            wait_units(slot, in_units)
             kv[chip, which, :, n * COLS:(n + 1) * COLS] = project(slot)
             slot += in_units
         two_step_start(*kv_ring, which)
@@ -315,15 +319,18 @@
 
     heads_chunk = COLS // HEAD_DIM
 
-    def q_step(n, carry):
-        res = project(lax.rem(kv_units + in_units * n, n_slots))
-        for i in range(heads_chunk):
-            q_buf[heads_chunk * n + i] = res[:, i * HEAD_DIM:(i + 1) * HEAD_DIM]
-
-        @pl.when(n < q_first)
-        def _():
-            for r in range(in_units):
-                start_o(early + in_units * n + r)
+    def q_step(m, carry):
+        first = lax.rem(kv_units + 2 * in_units * m, n_slots)
+        wait_units(first, 2 * in_units)
+        for half in range(2):
+            res = project(first + in_units * half)
+            for i in range(heads_chunk):
+                q_buf[heads_chunk * (2 * m + half) + i] = res[:, i * HEAD_DIM:(i + 1) * HEAD_DIM]
+
+        @pl.when(2 * m < q_first)
+        def _():
+            for r in range(2 * in_units):
+                start_o(early + 2 * in_units * m + r)
         return carry
 
     lax.fori_loop(0, Q_STOPS[0], q_step, 0)
@@ -333,9 +340,8 @@
     two_step_onward(*kv_ring, 0)
     lax.fori_loop(Q_STOPS[0], Q_STOPS[1], q_step, 0)
     two_step_onward(*kv_ring, 1)
+    lax.fori_loop(Q_STOPS[1], q_chunks // 2, q_step, 0)
     ring_hop(*tab_ring, 0, 0)
-    lax.fori_loop(Q_STOPS[1], q_chunks, q_step, 0)
-    ring_hop(*tab_ring, 0, 1)
     for which in range(2):
         two_step_last(*kv_ring, which)
 
@@ -360,7 +366,7 @@
         copy = remote(o_buf.at[0, :, span], o_buf.at[1, :, span], o_send.at[g], o_recv.at[g], partner)
         copy.start()
         o_copies.append(copy)
-    ring_hop(*tab_ring, 0, 2)
+    ring_hop(*tab_ring, 0, 1)
 
     h_ring = (h_piece, h_send, h_recv)
 
@@ -382,16 +388,13 @@
 
     def o_step(j, carry):
         at = first_o + chunk_units * j
-        for r in range(half_units):
-            wait_unit(at + r)
-        acc = jnp.dot(o_buf[0], wbuf[pl.ds(at, half_units)].reshape(q_core, COLS), preferred_element_type=jnp.float32)
 
         @pl.when(j == 0)
         def _():
             for copy in o_copies:
                 copy.wait_recv()
-        for r in range(half_units):
-            wait_unit(at + half_units + r)
+        wait_units(at, chunk_units)
+        acc = jnp.dot(o_buf[0], wbuf[pl.ds(at, half_units)].reshape(q_core, COLS), preferred_element_type=jnp.float32)
         acc += jnp.dot(o_buf[1], wbuf[pl.ds(at + half_units, half_units)].reshape(q_core, COLS), preferred_element_type=jnp.float32)
         x_cols = x_buf[:, pl.ds(pl.multiple_of(core * out_core + j * COLS, COLS), COLS)]
         h_all[chip, core * o_chunks + j] = (x_cols.astype(jnp.float32) + acc).astype(jnp.bfloat16)
@@ -409,6 +412,10 @@
             @pl.when((late >= 0) & (late < CHAIN))
             def _(late=late, reach=reach):
                 chain_hop(late, reach)
+
+        @pl.when(j == 3)
+        def _():
+            ring_hop(*tab_ring, 0, 2)
 
         @pl.when(j >= CHAIN + LAG)
         def _():
@@ -429,11 +436,8 @@
     table_out[...] = jnp.sum(tabs[...], axis=0)
     for j in range(CHAIN):
         chain_hop(j, fwd)
-    for j in range(max(CHAIN, o_chunks - 2 * LAG), o_chunks):
+    for j in range(max(CHAIN, o_chunks - 2 * LAG), o_chunks - 1):
         last_step(j)
-    for j in range(o_chunks):
-        h_pair(j, other).wait_recv()
-
     x_pair.wait_send()
     t_pair.wait_send()
     for back, hops in ((0, fwd), (1, bwd)):
@@ -443,13 +447,15 @@
         two_step_sent(*kv_ring, which)
     for copy in o_copies:
         copy.wait_send()
-
-    def sent(j, carry):
-        two_step_sent(*h_ring, j)
-        h_pair(j, core).wait_send()
-        return carry
-
-    lax.fori_loop(0, o_chunks, sent, 0)
+    lax.fori_loop(0, o_chunks - 1, lambda n, c: (two_step_sent(*h_ring, n), c)[1], 0)
+    last_step(o_chunks - 1)
+    for j in range(o_chunks):
+        h_pair(j, other).wait_recv()
+
+    for n in range(o_chunks - 1, o_chunks):
+        two_step_sent(*h_ring, n)
+    for n in range(o_chunks):
+        h_pair(n, core).wait_send()
 
 
 def attend(x_loc, w_q, w_k, w_v, w_o, ids, probs, group):

time: 61.2 us -> 62.1 us (1.015)
  Pallas kernels: 60.4 us -> 61.3 us
    pallas_call x1, Pallas kernels: 54.2 us -> 55.1 us  [attend(): pl.pallas_call(block_kernel, name='attend', in_specs=[anywhere] * 7, out_...]
where the time goes in v5:
time: 62.1 us; the launch traced here: 62 us
  Pallas kernels  61.3 us (99%)
  between operations  0.64 us (1%)
    pallas_call x1, Pallas kernels, attend(): pl.pallas_call(block_kernel, name='attend', in_specs=[anywhere] * 7, out_...  55.1 us
    pallas_call x1, Pallas kernels, build_buffers(): pl.pallas_call(build_kernel, name='build_buffers', in_specs=[in_vmem, in_...  6.23 us

profile of v5, /device:TPU:21, one launch (start us, length us, event | category | flops | bytes accessed | tf_op | source)
XLA Modules:
  0.0 62.0 jit_solution(6929038501185771412)
XLA Ops:
  0.6 55.1 %attend.1 = (bf16[8,16,32,256]{3,2,1,0:T(8,128)(2,1)S(1)}, f32[8,128]{1,0:T(8,128)S(1)}) custom-call(bf16[16,4096]{1,0:T(8,128)(2,1)} %x_hbm.1, bf16[4096,12288]{1,0:T(8,128)(2,1)} %wq.1, bf16[4096,1024]{1,0:T(8,128)(2,1)} %wk.1, bf16[4096,1024]{1,0:T(8,128)(2,1)} %wv.1, bf16[12288,4096]{1,0:T(8,128)(2,1)} %wo.1, s32[2,16]{1,0:T(2,128)} %bitcast.1, ...), custom_call_target="tpu_custom_call" | custom-call | tf_op jit(solution)/shard_map/attend/pallas_call | solution.py:479
  55.7 6.2 %build_buffers.1 = (bf16[8,256,4096]{2,1,0:T(8,128)(2,1)}, bf16[16,4096]{1,0:T(8,128)(2,1)}) custom-call(bf16[8,16,32,256]{3,2,1,0:T(8,128)(2,1)S(1)} %get-tuple-element.6.h_ref, f32[8,128]{1,0:T(8,128)S(1)} %get-tuple-element.7.table_ref), custom_call_target="tpu_custom_call" | custom-call | flops 4294967296 | bytes 16777216 | tf_op jit(solution)/shard_map/build_buffers/pallas_call | solution.py:136
